TPU v7x, 128 devices: a whole 4x4x4 slice. The times are simulated.
128 devices in a mesh: sub: 8 (over z, core), ma: 16 (over y, x).
Axes of the slice: x: 4, y: 4, z: 4, core: 2. Of those that a mesh axis runs over, the one named last changes fastest.
Arguments:
- forcing: float32 [2, 512, 2, 128, 512], P(None, 'sub', None, 'ma'), may hold values from -24 to 24
- slot_wavenumber: int32 [128], P('ma'), may hold values from 0 to 511, as said below
- inverse: float32 [8, 2, 64, 64, 512], P('sub'), may hold values from -2 to 2
- edge_weights: float32 [8, 2, 64], P('sub'), may hold values from -2908 to 2908, as said below
Outputs:
- transform_field: float32 [2, 512, 2, 128, 512], P(None, ('sub', 'ma'))
Inputs may be any that keep to these rules, and one draw needn't show every extreme that they name: `slot_wavenumber`: each device's slots hold 4 pairs: slots 2j and 2j + 1 carry a wavenumber m below 256 and 511 - m, in that order; no wavenumber appears twice. `edge_weights`: together with inverse it makes every row of the interface system strictly diagonally dominant with a positive diagonal.
All inputs are finite; a program needn't handle non-finite values.
Results may differ from a plain program's by a relative error of at most 0.0003.
Values sent between devices are 32-bit elements; how exact they have to be, the bound alone decides.
No kernel may reach another device: no remote copies, remote signals or barrier semaphores. Data moves between devices by JAX's collectives and lax.ppermute only.
A program may use at most 192 MiB of HBM per device.

v0:
```python
import math

import jax
import jax.numpy as jnp
from jax import lax
from jax.sharding import PartitionSpec as P

HIGH = lax.Precision.HIGHEST


def sent_to_all(shard, axis):
    copies = jnp.broadcast_to(shard, (lax.axis_size(axis), *shard.shape))
    return lax.all_to_all(copies, axis, split_axis=0, concat_axis=0, tiled=True)


def laid_out(tiles, dim):
    dims = list(tiles.shape[1:])
    dims[dim] *= tiles.shape[0]
    return jnp.moveaxis(tiles, 0, dim).reshape(dims)


def gather_directly(shard, axis, dim):
    tiles = sent_to_all(shard, axis)
    return laid_out(tiles, dim)


def in_one_piece(arrays, axis, dim, along):
    widths = [math.prod(a.shape[along:]) for a in arrays]
    both = jnp.concatenate(
        [a.reshape(*a.shape[:along], w) for a, w in zip(arrays, widths)], axis=along
    )
    out = gather_directly(both, axis, dim)
    tiles = jnp.split(out, [sum(widths[:k]) for k in range(1, len(widths))], axis=along)
    return tuple((b.reshape(*out.shape[:along], *a.shape[along:]) for a, b in zip(arrays, tiles)))


def widen(values):
    return values[:, None, None, :]


def body(forcing, slot_wavenumber, inverse, edge_weights):
    fields, points, halves, slot_count, degrees = forcing.shape
    block_inverse = inverse[0]
    edge_rows = edge_weights[0]
    degree = jnp.arange(degrees, dtype=jnp.int32)
    kept_modes = (degree[None, :] >= slot_wavenumber[:, None]).astype(jnp.float32)
    position = jnp.arange(points, dtype=jnp.int32)
    interior = ((position > 0) & (position < points - 1)).astype(jnp.float32)
    source = forcing * kept_modes[None, None, None, :, :] * interior[None, :, None, None, None]
    particular = jnp.einsum("fpql,fqcml->fpcml", block_inverse, source, precision=HIGH)
    low_slope = jnp.einsum("p,fpcml->fcml", edge_rows[0], particular, precision=HIGH)
    top_slope = jnp.einsum("p,fpcml->fcml", edge_rows[1], particular, precision=HIGH)
    lower_unit = block_inverse[:, :, 0, :]
    upper_unit = block_inverse[:, :, points - 1, :]
    low_influence = jnp.stack(
        [
            jnp.einsum("p,fpl->fl", edge_rows[0], lower_unit, precision=HIGH),
            jnp.einsum("p,fpl->fl", edge_rows[0], upper_unit, precision=HIGH),
        ]
    )
    top_influence = jnp.stack(
        [
            jnp.einsum("p,fpl->fl", edge_rows[1], lower_unit, precision=HIGH),
            jnp.einsum("p,fpl->fl", edge_rows[1], upper_unit, precision=HIGH),
        ]
    )
    sub_index = lax.axis_index("sub")
    gathered = in_one_piece(
        (top_slope[None], top_influence[None], low_slope[None], low_influence[None]), "sub", 0, 3
    )
    all_top_slope, all_top_influence, all_low_slope, all_low_influence = gathered
    lower_coefs = all_top_influence[:-1, 0]
    middle_coefs = all_top_influence[:-1, 1] - all_low_influence[1:, 0]
    upper_coefs = -all_low_influence[1:, 1]
    right_sides = all_low_slope[1:] - all_top_slope[:-1]

    def eliminate(state_pair, inputs):
        ratio_prev, reduced_prev = state_pair
        lower_here, middle_here, upper_here, right_here = inputs
        pivot_value = middle_here - lower_here * ratio_prev
        ratio_here = upper_here / pivot_value
        reduced_here = (right_here - widen(lower_here) * reduced_prev) / widen(pivot_value)
        return ((ratio_here, reduced_here), (ratio_here, reduced_here))

    initial = (jnp.zeros_like(lower_coefs[0]), jnp.zeros_like(right_sides[0]))
    _, (ratios, reduceds) = lax.scan(
        eliminate, initial, (lower_coefs, middle_coefs, upper_coefs, right_sides)
    )

    def substitute(later_value, inputs):
        ratio_here, reduced_here = inputs
        current = reduced_here - widen(ratio_here) * later_value
        return (current, current)

    _, interface = lax.scan(
        substitute, jnp.zeros_like(right_sides[0]), (ratios, reduceds), reverse=True
    )
    boundary = jnp.zeros_like(interface[:1])
    lower_value = lax.dynamic_index_in_dim(
        jnp.concatenate([boundary, interface]), sub_index, 0, keepdims=False
    )
    upper_value = lax.dynamic_index_in_dim(
        jnp.concatenate([interface, boundary]), sub_index, 0, keepdims=False
    )
    solution = particular + lower_value[:, None] * lower_unit[:, :, None, None, :]
    solution = solution + upper_value[:, None] * upper_unit[:, :, None, None, :]
    return lax.all_to_all(solution, "ma", split_axis=1, concat_axis=3, tiled=True)


def solution(mesh):
    return jax.shard_map(
        body,
        mesh=mesh,
        in_specs=(
            P(None, "sub", None, "ma", None),
            P("ma"),
            P("sub", None, None, None, None),
            P("sub", None, None),
        ),
        out_specs=P(None, ("sub", "ma"), None, None, None),
        check_vma=False,
    )
```

profile of v0, /device:TPU:1, one launch (start us, length us, event | category | flops | bytes accessed | tf_op | source)
XLA Modules:
  0.0 233.1 jit_solution(1013579382292759196)
XLA Ops:
  0.0 2.7 %fusion.34 = (f32[2,64,1,512]{3,2,1,0:T(1,128)S(1)}, f32[2,64,1,512]{3,2,1,0:T(1,128)S(1)}) fusion(f32[2,64,64,512]{3,2,1,0:T(8,128)} %bitcast.121), kind=kLoop, calls=%fused_computation.59 | loop fusion | bytes 1048576 | tf_op jit(solution)/shard_map/slice | solution.py:53
  2.8 0.9 fusion.4
  3.7 0.9 fusion.2
  4.6 0.9 fusion.8
  5.5 0.9 fusion.6
  6.4 0.7 fusion.18
  7.2 4.6 %multiply_multiply_fusion = f32[2,64,2,8,512]{4,3,2,1,0:T(8,128)} fusion(f32[2,64,2,8,512]{4,3,2,1,0:T(8,128)} %param.8, f32[64]{0:T(128)S(1)} %and_convert_fusion, f32[8,512]{1,0:T(8,128)S(1)} %fusion.18), kind=kLoop, calls=%fused_computation.16 | loop fusion | flops 2097152 | bytes 8405248 | tf_op jit(solution)/shard_map/mul | solution.py:49
  11.8 8.7 %copy.30 = f32[2,64,2,8,512]{1,3,2,4,0:T(8,128)} copy(f32[2,64,2,8,512]{4,3,2,1,0:T(8,128)} %multiply_multiply_fusion) | data formatting | bytes 8388608 | tf_op jit(solution)/shard_map/mul | solution.py:49
  20.4 30.5 %copy.40 = f32[2,64,64,512,1]{2,1,4,3,0:T(8,128)} copy(f32[2,64,64,512,1]{3,2,1,0,4:T(8,128)} %bitcast.122) | data formatting | bytes 33554432 | tf_op jit(solution)/shard_map/squeeze | solution.py:43
  51.0 57.6 %fusion.35 = f32[2,512,2,8,64]{4,3,2,1,0:T(8,128)} fusion(f32[2,64,2,8,512]{1,3,2,4,0:T(8,128)} %copy.30, f32[2,64,64,512,1]{2,1,4,3,0:T(8,128)} %copy.40), kind=kOutput, calls=%fused_computation.60 | convolution fusion | flops 805306368 | bytes 25165824 | tf_op jit(solution)/shard_map/fpql,fqcml->fpcml/dot_general | solution.py:50
  108.6 7.6 %copy.32 = f32[2,2,8,512,64]{3,2,4,1,0:T(8,128)} copy(f32[2,2,8,512,64]{4,2,1,3,0:T(8,128)} %bitcast.120) | data formatting | bytes 8388608 | tf_op jit(solution)/shard_map/p,fpcml->fcml/dot_general | solution.py:52
  116.2 5.0 %reshape.63 = f32[2,2,4096,64]{2,3,1,0:T(8,128)} reshape(f32[2,2,8,512,64]{3,2,4,1,0:T(8,128)} %copy.32) | data formatting | bytes 8388608 | tf_op jit(solution)/shard_map/reshape.50
  121.2 4.5 %fusion.21 = f32[1,2,2,4096]{3,0,2,1:T(1,128)S(1)} fusion(f32[2,2,4096,64]{2,3,1,0:T(8,128)} %reshape.63, f32[1,2,64]{2,1,0:T(2,128)S(1)} %copy-done), kind=kOutput, calls=%fused_computation.47 | convolution fusion | flops 12582912 | bytes 4260352 | tf_op jit(solution)/shard_map/p,fpcml->fcml/dot_general | solution.py:51
  125.6 4.5 %fusion.25 = f32[1,2,2,4096]{3,0,2,1:T(1,128)S(1)} fusion(f32[2,2,4096,64]{2,3,1,0:T(8,128)} %reshape.63, f32[1,2,64]{2,1,0:T(2,128)S(1)} %copy-done), kind=kOutput, calls=%fused_computation.51 | convolution fusion | flops 12582912 | bytes 4260352 | tf_op jit(solution)/shard_map/p,fpcml->fcml/dot_general | solution.py:52
  130.4 1.3 broadcast_in_dim.46
  131.7 6.8 %all-to-all-start = ((f32[8,1,2,2,9216]{4,3,2,1,0:T(2,128)}), f32[8,1,2,2,9216]{4,3,2,1,0:T(2,128)S(1)}, u32[]{:S(2)}, u32[]{:S(2)}) async-start(f32[8,1,2,2,9216]{4,3,2,1,0:T(2,128)} %broadcast_in_dim.46), calls=%async_computation | async-start | bytes 2359296 | tf_op jit(solution)/shard_map/all_to_all | solution.py:13
  138.9 15.9 %all-to-all-done = f32[8,1,2,2,9216]{4,3,2,1,0:T(2,128)S(1)} async-done(((f32[8,1,2,2,9216]{4,3,2,1,0:T(2,128)}), f32[8,1,2,2,9216]{4,3,2,1,0:T(2,128)S(1)}, u32[]{:S(2)}, u32[]{:S(2)}) %all-to-all-start) | async-done | bytes 1179680 | tf_op jit(solution)/shard_map/all_to_all | solution.py:13
  155.6 0.5 while.34
  156.7 0.5 copy.35
  157.3 0.5 copy.33
  157.8 8.6 %fusion.1 = f32[2,64,2,8,512]{1,3,2,4,0:T(8,128)} fusion(f32[2,512,2,8,64]{4,3,2,1,0:T(8,128)} %fusion.35, f32[2,64,512]{1,2,0:T(8,128)S(1)} %bitcast.126, f32[2,2,8,512]{2,1,3,0:T(2,128)S(1)} %copy.35, f32[2,64,512]{1,2,0:T(8,128)S(1)} %bitcast.127, f32[2,2,8,512]{2,1,3,0:T(2,128)S(1)} %copy.33), kind=kLoop, calls=%fused_computation.14 | loop fusion | flops 4194304 | bytes 9043968 | tf_op jit(solution)/shard_map/add | solution.py:106
  166.4 7.6 %copy.37 = f32[2,64,2,8,512]{4,3,2,0,1:T(8,128)} copy(f32[2,64,2,8,512]{1,3,2,4,0:T(8,128)} %fusion.1) | data formatting | bytes 8388608 | tf_op jit(solution)/shard_map/add | solution.py:106
  174.0 56.5 %all_to_all.23 = f32[2,64,2,8,512]{4,3,2,0,1:T(8,128)S(1)} all-to-all(f32[2,64,2,8,512]{4,3,2,0,1:T(8,128)} %copy.37), channel_id=1, replica_groups=mesh['sub'=8,'ma'=16] {'ma'}, dimensions={1} | all-to-all | bytes 8388608 | tf_op jit(solution)/shard_map/all_to_all | solution.py:107
  230.5 2.7 %copy.73 = f32[2,4,2,16,8,512]{5,4,3,2,1,0:T(8,128)} copy(f32[2,4,2,16,8,512]{5,4,2,0,1,3:T(8,128)S(1)} %bitcast.123) | data formatting | bytes 8388608 | tf_op jit(solution)/shard_map/all_to_all | solution.py:107
  (52 shorter events, 2.5 us)
Async XLA Ops:
  108.6 12.6 %copy-start = (f32[1,2,64]{2,1,0:T(2,128)S(1)}, f32[1,2,64]{2,1,0:T(2,128)}, u32[]{:S(2)}) copy-start(f32[1,2,64]{2,1,0:T(2,128)} %param.11) | copy-start | bytes 1540
  131.7 23.2 %all-to-all-start = ((f32[8,1,2,2,9216]{4,3,2,1,0:T(2,128)}), f32[8,1,2,2,9216]{4,3,2,1,0:T(2,128)S(1)}, u32[]{:S(2)}, u32[]{:S(2)}) async-start(f32[8,1,2,2,9216]{4,3,2,1,0:T(2,128)} %broadcast_in_dim.46), calls=%async_computation | async-start | bytes 2359296 | tf_op jit(solution)/shard_map/all_to_all | solution.py:13
where the time goes:
time: 235 us; the launch traced here: 233 us
  matrix products  70.3 us (30%)
  local copies, waits for them, and re-layouts  68.2 us (29%)
  blocking collectives  56.5 us (24%)
  waiting for transfers between devices  15.9 us (7%)
  other arithmetic  14.9 us (6%)
  starting transfers between devices  6.8 us (3%)
    dot_general x1, matrix products, body(): jnp.einsum('fpql,fqcml->fpcml', block_inverse, source, precision=HIGH)  57.6 us
    all_to_all x1, blocking collectives, body(): lax.all_to_all(solution, 'ma', split_axis=1, concat_axis=3, tiled=True)  56.5 us
    squeeze x1, local copies, waits for them, and re-layouts, body(): block_inverse = inverse[0]  30.5 us
    all_to_all x1, waiting for transfers between devices, sent_to_all(): return lax.all_to_all(copies, axis, split_axis=0, concat_axis=0, tiled=True)  15.9 us
    mul x1, local copies, waits for them, and re-layouts, body(): forcing * kept_modes[None, None, None, :, :]  8.66 us
    add x1, other arithmetic, body(): solution = solution + upper_value[:, None] * upper_unit[:, :, None, None, :]  8.58 us
    dot_general x2, local copies, waits for them, and re-layouts, body(): jnp.einsum('p,fpcml->fcml', edge_rows[1], particular, precision=HIGH)  7.68 us
    add x1, local copies, waits for them, and re-layouts, body(): solution = solution + upper_value[:, None] * upper_unit[:, :, None, None, :]  7.61 us
  transfers between devices with their start and end apart: 1, of which 1 were waited for; matrix products, arithmetic and copies ran while one was open for 0% of the time, Pallas kernels for 0%

commit v1 on v0

v1 whole, which is shorter than its diff:
```python
import jax
import jax.numpy as jnp
from jax import lax
from jax.experimental import pallas as pl
from jax.experimental.pallas import tpu as pltpu
from jax.sharding import PartitionSpec as P

F32 = jnp.float32
POINTS = 64
FIELDS = 2
NSUB = 8
GROUPS = 16
LANES = 128
ROWS = 8
PACK = 5
QB = 8
PB = 8
NEAR = POINTS // GROUPS
SLOPES = 2 * FIELDS * PACK
MESSAGE = SLOPES + 4
SENT = FIELDS * NEAR * 4 + 1


def lane_iota():
    return lax.broadcasted_iota(jnp.int32, (ROWS, LANES), 1)


def row_iota():
    return lax.broadcasted_iota(jnp.int32, (ROWS, LANES), 0)


def pair_wavenumber(slot_ref):
    pair = row_iota() // 2
    m = jnp.full((ROWS, LANES), slot_ref[0], jnp.int32)
    for j in range(1, 4):
        m = jnp.where(pair == j, slot_ref[2 * j], m)
    return m


def down(x):
    return pltpu.roll(x, 1, 0)


def up(x):
    return pltpu.roll(x, ROWS - 1, 0)


def slope_kernel(slot_ref, weight_ref, inv_ref, src_ref, packed_ref, msg_ref, e_ref):
    f = pl.program_id(0)
    block = pl.program_id(1)
    m = pair_wavenumber(slot_ref)
    lane = lane_iota()
    row = row_iota()
    even = row % 2 == 0
    small = m < LANES
    keep1 = lane + LANES >= m
    keep3 = lane + 3 * LANES >= jnp.where(even, m, 511 - m)
    keep_mix = lane >= jnp.where(small, m, 255 - m)

    def gather_rows(p, carry):
        out = []
        low = weight_ref[0, 0, p]
        top = weight_ref[0, 1, p]
        for b in range(4):
            tile = inv_ref[0, p, :, b * LANES:(b + 1) * LANES]
            out.append(carry[2 * b] + low * tile)
            out.append(carry[2 * b + 1] + top * tile)
        return tuple(out)

    zero = jnp.zeros((QB, LANES), F32)
    rows = lax.fori_loop(0, POINTS, gather_rows, (zero,) * 8, unroll=8)
    for b in range(4):
        e_ref[0, b] = rows[2 * b]
        e_ref[1, b] = rows[2 * b + 1]

    @pl.when(block == 0)
    def _():
        for r in range(2):
            for v in range(PACK):
                msg_ref[(r * FIELDS + f) * PACK + v] = jnp.zeros((ROWS, LANES), F32)
            for b in range(4):
                msg_ref[SLOPES + b, pl.ds(r * 4 + f * 2, 1), :] = e_ref[r, b, 0:1, :]

    @pl.when(block == POINTS // QB - 1)
    def _():
        for r in range(2):
            for b in range(4):
                msg_ref[SLOPES + b, pl.ds(r * 4 + f * 2 + 1, 1), :] = e_ref[r, b, QB - 1:QB, :]

    sums = [[msg_ref[(r * FIELDS + f) * PACK + v] for v in range(PACK)] for r in range(2)]
    for q in range(QB):
        point = block * QB + q
        inside = jnp.logical_and(point > 0, point < POINTS - 1).astype(F32)
        s = [[src_ref[0, q, c, :, b * LANES:(b + 1) * LANES] for b in range(4)] for c in range(2)]
        first = jnp.where(even, s[0][0], down(s[1][0]))
        late = jnp.where(even, up(s[0][2]), s[1][2])
        vectors = [
            jnp.where(keep1, jnp.where(even, s[0][1], down(s[1][1])), 0.0),
            jnp.where(even, s[0][2], down(s[1][2])),
            jnp.where(keep3, s[0][3], 0.0),
            jnp.where(keep3, s[1][3], 0.0),
            jnp.where(keep_mix, jnp.where(small, first, late), 0.0),
        ]
        vectors = [v * inside for v in vectors]
        for v in range(PACK):
            packed_ref[0, q, v] = vectors[v]
        for r in range(2):
            e = [e_ref[r, b, pl.ds(q, ROWS, stride=0), :] for b in range(4)]
            e = [e[1], e[2], e[3], e[3], jnp.where(small, e[0], e[2])]
            for v in range(PACK):
                sums[r][v] = sums[r][v] + e[v] * vectors[v]
    for r in range(2):
        for v in range(PACK):
            msg_ref[(r * FIELDS + f) * PACK + v] = sums[r][v]


def slopes(slot, weights, inverse, forcing):
    return pl.pallas_call(
        slope_kernel,
        grid=(FIELDS, POINTS // QB),
        in_specs=[
            pl.BlockSpec(memory_space=pltpu.SMEM),
            pl.BlockSpec(memory_space=pltpu.SMEM),
            pl.BlockSpec((1, POINTS, QB, 512), lambda f, q: (f, 0, q, 0)),
            pl.BlockSpec((1, QB, 2, ROWS, 512), lambda f, q: (f, q, 0, 0, 0)),
        ],
        out_specs=[
            pl.BlockSpec((1, QB, PACK, ROWS, LANES), lambda f, q: (f, q, 0, 0, 0)),
            pl.BlockSpec((MESSAGE, ROWS, LANES), lambda f, q: (0, 0, 0)),
        ],
        out_shape=[
            jax.ShapeDtypeStruct((FIELDS, POINTS, PACK, ROWS, LANES), F32),
            jax.ShapeDtypeStruct((MESSAGE, ROWS, LANES), F32),
        ],
        scratch_shapes=[pltpu.VMEM((2, 4, QB, LANES), F32)],
        compiler_params=pltpu.CompilerParams(dimension_semantics=("arbitrary", "arbitrary")),
        cost_estimate=pl.CostEstimate(flops=20_000_000, bytes_accessed=24_000_000, transcendentals=0),
        name="slopes",
    )(slot, weights, inverse, forcing)


def solve_kernel(slot_ref, inv_ref, src_ref, part_ref, edge_ref):
    small = pair_wavenumber(slot_ref) < LANES

    def unit(p, block, r, b):
        line = inv_ref[0, p, block, r:r + 1, b * LANES:(b + 1) * LANES]
        return jnp.broadcast_to(line, (ROWS, LANES))

    def odd_pass(block, sums):
        sums = list(sums)
        for r in range(ROWS):
            s = [src_ref[0, block, r, v] for v in (0, 2, 3)]
            for p in range(PB):
                one = unit(p, block, r, 1)
                three = unit(p, block, r, 3)
                sums[3 * p] = sums[3 * p] + one * s[0]
                sums[3 * p + 1] = sums[3 * p + 1] + three * s[1]
                sums[3 * p + 2] = sums[3 * p + 2] + three * s[2]
        return tuple(sums)

    def even_pass(block, sums):
        sums = list(sums)
        for r in range(ROWS):
            s = [src_ref[0, block, r, v] for v in (1, 4)]
            for p in range(PB):
                none = unit(p, block, r, 0)
                two = unit(p, block, r, 2)
                sums[2 * p] = sums[2 * p] + two * s[0]
                sums[2 * p + 1] = sums[2 * p + 1] + jnp.where(small, none, two) * s[1]
        return tuple(sums)

    zero = jnp.zeros((ROWS, LANES), F32)
    sums = lax.fori_loop(0, POINTS // ROWS, odd_pass, (zero,) * (3 * PB))
    for p in range(PB):
        part_ref[0, p, 0] = sums[3 * p]
        part_ref[0, p, 2] = sums[3 * p + 1]
        part_ref[0, p, 3] = sums[3 * p + 2]
    sums = lax.fori_loop(0, POINTS // ROWS, even_pass, (zero,) * (2 * PB))
    for p in range(PB):
        part_ref[0, p, 1] = sums[2 * p]
        part_ref[0, p, 4] = sums[2 * p + 1]
        for b in range(4):
            lanes = slice(b * LANES, (b + 1) * LANES)
            edge_ref[0, p, 2 * b:2 * b + 1, :] = inv_ref[0, p, 0, 0:1, lanes]
            edge_ref[0, p, 2 * b + 1:2 * b + 2, :] = inv_ref[0, p, POINTS // ROWS - 1, ROWS - 1:ROWS, lanes]


def particular(slot, inverse, packed):
    return pl.pallas_call(
        solve_kernel,
        grid=(FIELDS, POINTS // PB),
        in_specs=[
            pl.BlockSpec(memory_space=pltpu.SMEM),
            pl.BlockSpec((1, PB, POINTS // ROWS, ROWS, 512), lambda f, p: (f, p, 0, 0, 0)),
            pl.BlockSpec((1, POINTS // ROWS, ROWS, PACK, ROWS, LANES), lambda f, p: (f, 0, 0, 0, 0, 0)),
        ],
        out_specs=[
            pl.BlockSpec((1, PB, PACK, ROWS, LANES), lambda f, p: (f, p, 0, 0, 0)),
            pl.BlockSpec((1, PB, ROWS, LANES), lambda f, p: (f, p, 0, 0)),
        ],
        out_shape=[
            jax.ShapeDtypeStruct((FIELDS, POINTS, PACK, ROWS, LANES), F32),
            jax.ShapeDtypeStruct((FIELDS, POINTS, ROWS, LANES), F32),
        ],
        compiler_params=pltpu.CompilerParams(dimension_semantics=("arbitrary", "arbitrary")),
        cost_estimate=pl.CostEstimate(flops=90_000_000, bytes_accessed=24_000_000, transcendentals=0),
        name="particular",
    )(
        slot,
        inverse.reshape(FIELDS, POINTS, POINTS // ROWS, ROWS, 512),
        packed.reshape(FIELDS, POINTS // ROWS, ROWS, PACK, ROWS, LANES),
    )


DEST = 4


def pack_kernel(slot_ref, *refs):
    blocks = refs[:NSUB]
    part_ref, edge_ref, out_ref, all_ref, u_ref = refs[NSUB:]
    sub = lax.axis_index("sub")
    m = pair_wavenumber(slot_ref)
    lane = lane_iota()
    row = row_iota()
    even = row % 2 == 0
    small = m < LANES

    @pl.when(pl.program_id(0) == 0)
    def _():
        for k in range(NSUB):
            place = lax.rem(sub + (NSUB - k), NSUB)
            for i in range(MESSAGE):
                all_ref[place, i] = blocks[k][i]
        zero = jnp.zeros((ROWS, LANES), F32)
        for f in range(FIELDS):
            for v in range(PACK):
                u_ref[0, f, v] = zero
                u_ref[NSUB, f, v] = zero

            def coefficient(t, r, k, b):
                return all_ref[t, SLOPES + b, pl.ds(r * 4 + f * 2 + k, ROWS, stride=0), :]

            ratio = [zero] * PACK
            reduced = [zero] * PACK
            ratios = []
            reduceds = []
            for level in range(NSUB - 1):
                factors = []
                for b in range(4):
                    lower = coefficient(level, 1, 0, b)
                    middle = coefficient(level, 1, 1, b) - coefficient(level + 1, 0, 0, b)
                    upper = -coefficient(level + 1, 0, 1, b)
                    factors.append((lower, middle, upper))
                mixed = tuple(jnp.where(small, x, y) for x, y in zip(factors[0], factors[2]))
                new_ratio, new_reduced = [None] * PACK, [None] * PACK
                for v, (lower, middle, upper) in enumerate((factors[1], factors[2], factors[3], factors[3], mixed)):
                    right = (
                        all_ref[level + 1, f * PACK + v]
                        - all_ref[level, (FIELDS + f) * PACK + v]
                    )
                    if v == 3:
                        inverted = last
                    else:
                        inverted = 1.0 / (middle - lower * ratio[v])
                    last = inverted
                    new_ratio[v] = upper * inverted
                    new_reduced[v] = (right - lower * reduced[v]) * inverted
                ratio, reduced = new_ratio, new_reduced
                ratios.append(ratio)
                reduceds.append(reduced)
            later = [zero] * PACK
            for level in range(NSUB - 2, -1, -1):
                later = [reduceds[level][v] - ratios[level][v] * later[v] for v in range(PACK)]
                for v in range(PACK):
                    u_ref[level + 1, f, v] = later[v]

    shift = jnp.where(small, m, m - LANES)
    turn = (lane - shift + LANES) % LANES
    below = lane < shift
    extra_at = LANES - 1 - shift
    for d in range(DEST):
        extra = jnp.where(lane == FIELDS * NEAR, m.astype(F32), 0.0)
        for f in range(FIELDS):
            u_low = [u_ref[sub, f, v] for v in range(PACK)]
            u_top = [u_ref[sub + 1, f, v] for v in range(PACK)]
            for k in range(NEAR):
                p = d * NEAR + k
                low = [edge_ref[f, p, pl.ds(2 * b, ROWS, stride=0), :] for b in range(4)]
                top = [edge_ref[f, p, pl.ds(2 * b + 1, ROWS, stride=0), :] for b in range(4)]
                low = [low[1], low[2], low[3], low[3], jnp.where(small, low[0], low[2])]
                top = [top[1], top[2], top[3], top[3], jnp.where(small, top[0], top[2])]
                x = [
                    part_ref[f, p, v] + u_low[v] * low[v] + u_top[v] * top[v] for v in range(PACK)
                ]
                low3 = jnp.where(even, x[2], down(x[3]))
                high3 = jnp.where(even, up(x[2]), x[3])
                mix = x[4]
                high3_t = jnp.take_along_axis(high3, turn, axis=1)
                mix_t = jnp.take_along_axis(mix, turn, axis=1)
                at = (f * NEAR + k) * 4
                out_ref[d, at] = jnp.where(
                    small,
                    jnp.where(below, high3_t, mix),
                    jnp.where(below, mix_t, high3_t),
                )
                out_ref[d, at + 1] = jnp.where(jnp.logical_and(below, jnp.logical_not(small)), high3_t, x[0])
                out_ref[d, at + 2] = x[1]
                out_ref[d, at + 3] = low3
                single = jnp.take_along_axis(jnp.where(small, high3, mix), extra_at, axis=1)
                extra = jnp.where(lane == f * NEAR + k, single, extra)
        out_ref[d, SENT - 1] = extra


def pack(slot, blocks, part, edges):
    return pl.pallas_call(
        pack_kernel,
        grid=(GROUPS // DEST,),
        in_specs=[pl.BlockSpec(memory_space=pltpu.SMEM)]
        + [pl.BlockSpec((MESSAGE, ROWS, LANES), lambda d: (0, 0, 0))] * NSUB
        + [
            pl.BlockSpec((FIELDS, DEST * NEAR, PACK, ROWS, LANES), lambda d: (0, d, 0, 0, 0)),
            pl.BlockSpec((FIELDS, DEST * NEAR, ROWS, LANES), lambda d: (0, d, 0, 0)),
        ],
        out_specs=pl.BlockSpec((DEST, SENT, ROWS, LANES), lambda d: (d, 0, 0, 0)),
        out_shape=jax.ShapeDtypeStruct((GROUPS, SENT, ROWS, LANES), F32),
        scratch_shapes=[
            pltpu.VMEM((NSUB, MESSAGE, ROWS, LANES), F32),
            pltpu.VMEM((NSUB + 1, FIELDS, PACK, ROWS, LANES), F32),
        ],
        compiler_params=pltpu.CompilerParams(dimension_semantics=("arbitrary",)),
        name="pack",
    )(slot, *blocks, part, edges)


FROM = 4


def unpack_kernel(in_ref, out_ref):
    lane = lane_iota()
    even = row_iota() % 2 == 0
    zero = jnp.zeros((ROWS, LANES), F32)
    for g in range(FROM):
        extras = in_ref[g, SENT - 1]
        m = jnp.take_along_axis(extras, jnp.full((ROWS, LANES), FIELDS * NEAR, jnp.int32), axis=1).astype(jnp.int32)
        small = m < LANES
        shift = jnp.where(small, m, m - LANES)
        back = (lane + shift) % LANES
        after = lane >= LANES - shift
        exact = lane == LANES - 1 - shift
        own0 = lane >= m
        own1 = lane + LANES >= m
        at_rows = pl.ds(g * ROWS, ROWS)
        for f in range(FIELDS):
            for k in range(NEAR):
                at = (f * NEAR + k) * 4
                s = [in_ref[g, at + b] for b in range(4)]
                single = jnp.take_along_axis(extras, jnp.full((ROWS, LANES), f * NEAR + k, jnp.int32), axis=1)
                g0 = jnp.take_along_axis(s[0], back, axis=1)
                g1 = jnp.take_along_axis(s[1], back, axis=1)
                value = jnp.where(after, g0, jnp.where(exact, single, 0.0))
                high3 = jnp.where(small, value, jnp.where(after, g1, g0))
                high2 = jnp.where(small, 0.0, value)
                low0 = jnp.where(own0, s[0], 0.0)
                low1 = jnp.where(own1, s[1], 0.0)
                lows = [low0, low1, s[2], s[3]]
                highs = [zero, zero, high2, high3]
                for b in range(4):
                    lanes = slice(b * LANES, (b + 1) * LANES)
                    high_first = highs[b] if b < 2 else down(highs[b])
                    out_ref[f, k, 0, at_rows, lanes] = jnp.where(even, lows[b], high_first)
                    out_ref[f, k, 1, at_rows, lanes] = jnp.where(even, up(lows[b]), highs[b])


def unpack(received):
    return pl.pallas_call(
        unpack_kernel,
        grid=(GROUPS // FROM,),
        in_specs=[pl.BlockSpec((FROM, SENT, ROWS, LANES), lambda g: (g, 0, 0, 0))],
        out_specs=pl.BlockSpec((FIELDS, NEAR, 2, FROM * ROWS, 512), lambda g: (0, 0, 0, g, 0)),
        out_shape=jax.ShapeDtypeStruct((FIELDS, NEAR, 2, GROUPS * ROWS, 512), F32),
        compiler_params=pltpu.CompilerParams(dimension_semantics=("arbitrary",)),
        name="unpack",
    )(received)


def body(forcing, slot_wavenumber, inverse, edge_weights):
    packed, message = slopes(slot_wavenumber, edge_weights, inverse[0], forcing)
    blocks = [message]
    for k in range(1, NSUB):
        blocks.append(lax.ppermute(message, "sub", [(i, (i + k) % NSUB) for i in range(NSUB)]))
    part, edges = particular(slot_wavenumber, inverse[0], packed)
    sent = pack(slot_wavenumber, blocks, part, edges)
    sent = sent.reshape(GROUPS, SENT * ROWS, LANES)
    received = lax.all_to_all(sent, "ma", split_axis=0, concat_axis=0, tiled=True)
    return unpack(received.reshape(GROUPS, SENT, ROWS, LANES))


def solution(mesh):
    return jax.shard_map(
        body,
        mesh=mesh,
        in_specs=(
            P(None, "sub", None, "ma", None),
            P("ma"),
            P("sub", None, None, None, None),
            P("sub", None, None),
        ),
        out_specs=P(None, ("sub", "ma"), None, None, None),
        check_vma=False,
    )
```

time: 235 us -> 95.1 us (0.40)
  the two profiles are of different devices: /device:TPU:1 before, /device:TPU:96 now
where the time goes in v1:
time: 95.1 us; the launch traced here: 94 us
  Pallas kernels  44.4 us (47%)
  blocking collectives  36 us (38%)
  starting transfers between devices  6.67 us (7%)
  waiting for transfers between devices  6.08 us (6%)
    all_to_all x1, blocking collectives, body(): lax.all_to_all(sent, 'ma', split_axis=0, concat_axis=0, tiled=True)  36 us
    pallas_call x1, Pallas kernels, particular(): pl.pallas_call(solve_kernel, grid=(FIELDS, POINTS // PB), in_specs=[pl.Bl...  20.2 us
    pallas_call x1, Pallas kernels, slopes(): pl.pallas_call(slope_kernel, grid=(FIELDS, POINTS // QB), in_specs=[pl.Bl...  14.8 us
    ppermute x7, starting transfers between devices, body(): lax.ppermute(message, 'sub', [(i, (i + k) % NSUB) for i in range(NSUB)])  6.67 us
    ppermute x7, waiting for transfers between devices, body(): lax.ppermute(message, 'sub', [(i, (i + k) % NSUB) for i in range(NSUB)])  6.08 us
    pallas_call x1, Pallas kernels, pack(): pl.pallas_call(pack_kernel, grid=(GROUPS // DEST,), in_specs=[pl.BlockSpe...  4.82 us
    pallas_call x1, Pallas kernels, unpack(): pl.pallas_call(unpack_kernel, grid=(GROUPS // FROM,), in_specs=[pl.BlockS...  4.66 us
  transfers between devices with their start and end apart: 7, of which 1 were waited for; matrix products, arithmetic and copies ran while one was open for 0% of the time, Pallas kernels for 21%

profile of v1, /device:TPU:96, one launch (start us, length us, event | category | flops | bytes accessed | tf_op | source)
XLA Modules:
  0.0 94.0 jit_solution(7415395385843356113)
XLA Ops:
  0.0 14.8 %slopes.1 = (f32[2,64,5,8,128]{4,3,2,1,0:T(8,128)}, f32[24,8,128]{2,1,0:T(8,128)}) custom-call(s32[8]{0:T(128)} %slot_ref.5, f32[1,2,64]{2,1,0:T(2,128)} %weight_ref.1, f32[2,64,64,512]{3,2,1,0:T(8,128)} %bitcast.5, f32[2,64,2,8,512]{4,3,2,1,0:T(8,128)} %src_ref.1), custom_call_target="tpu_custom_call" | custom-call | flops 20000000 | bytes 24000000 | tf_op jit(solution)/shard_map/slopes/pallas_call | solution.py:118
  14.8 0.0 collective-permute-start.6
  14.8 0.5 collective-permute-start.5
  15.2 0.2 collective-permute-start.4
  15.4 3.5 %collective-permute-start.3 = (f32[24,8,128]{2,1,0:T(8,128)}, f32[24,8,128]{2,1,0:T(8,128)S(1)}, u32[]{:S(2)}, u32[]{:S(2)}) collective-permute-start(f32[24,8,128]{2,1,0:T(8,128)} %get-tuple-element.9.refs_0_), channel_id=1, source_target_pairs={{0,64},{16,80},{32,96},{48,112},{64,0},{80,16},{96,32},{112,48},{1... | collective-permute-start | bytes 294920 | tf_op jit(solution)/shard_map/ppermute | solution.py:390
  18.9 2.1 %collective-permute-start.2 = (f32[24,8,128]{2,1,0:T(8,128)}, f32[24,8,128]{2,1,0:T(8,128)S(1)}, u32[]{:S(2)}, u32[]{:S(2)}) collective-permute-start(f32[24,8,128]{2,1,0:T(8,128)} %get-tuple-element.9.refs_0_), channel_id=1, source_target_pairs={{0,48},{16,64},{32,80},{48,96},{64,112},{80,0},{96,16},{112,32},{1... | collective-permute-start | bytes 294920 | tf_op jit(solution)/shard_map/ppermute | solution.py:390
  21.0 0.0 collective-permute-done.6.refs_7_
  21.0 0.5 collective-permute-start.1
  21.5 6.1 %collective-permute-done.5.refs_6_ = f32[24,8,128]{2,1,0:T(8,128)S(1)} collective-permute-done((f32[24,8,128]{2,1,0:T(8,128)}, f32[24,8,128]{2,1,0:T(8,128)S(1)}, u32[]{:S(2)}, u32[]{:S(2)}) %collective-permute-start.5) | collective-permute-done | bytes 98336 | tf_op jit(solution)/shard_map/ppermute | solution.py:390
  27.5 0.0 collective-permute-start
  27.5 20.2 %particular.1 = (f32[2,64,5,8,128]{4,3,2,1,0:T(8,128)}, f32[2,64,8,128]{3,2,1,0:T(8,128)}) custom-call(s32[8]{0:T(128)} %slot_ref.5, f32[2,64,8,8,512]{4,3,2,1,0:T(8,128)} %bitcast.6, f32[2,8,8,5,8,128]{5,4,3,2,1,0:T(8,128)} %bitcast.9), custom_call_target="tpu_custom_call" | custom-call | flops 90000000 | bytes 24000000 | tf_op jit(solution)/shard_map/particular/pallas_call | solution.py:189
  47.7 0.0 collective-permute-done.4.refs_5_
  47.7 0.0 collective-permute-done.3.refs_4_
  47.8 0.0 collective-permute-done.2.refs_3_
  47.8 0.0 collective-permute-done.1.refs_2_
  47.8 0.0 collective-permute-done.refs_1_
  47.8 0.5 copy-done.2
  48.4 0.0 copy-done.3
  48.4 0.0 copy-done.4
  48.5 0.0 copy-done.5
  48.5 0.0 copy-done.6
  48.5 4.8 %pack.1 = f32[16,33,8,128]{3,2,1,0:T(8,128)} custom-call(s32[8]{0:T(128)} %slot_ref.5, f32[24,8,128]{2,1,0:T(8,128)} %get-tuple-element.9.refs_0_, f32[24,8,128]{2,1,0:T(8,128)} %copy-done.6, f32[24,8,128]{2,1,0:T(8,128)} %copy-done.5, f32[24,8,128]{2,1,0:T(8,128)} %copy-done.4, f32[24,8,128]{2,1,0:T(8,128)} %copy-done.3, f32[24,8,128]{2,1,0:T(8,128)} %copy-done.2, ...), custom_call_target="tpu_custom_call" | custom-call | tf_op jit(solution)/shard_map/pack/pallas_call | solution.py:315
  53.3 36.0 %all_to_all.5 = f32[16,264,128]{2,1,0:T(8,128)} all-to-all(f32[16,264,128]{2,1,0:T(8,128)} %bitcast.7), channel_id=1, replica_groups=mesh['sub'=8,'ma'=16] {'ma'}, dimensions={0} | all-to-all | bytes 4325376 | tf_op jit(solution)/shard_map/all_to_all | solution.py:394
  89.4 4.7 %unpack.1 = f32[2,4,2,128,512]{4,3,2,1,0:T(8,128)} custom-call(f32[16,33,8,128]{3,2,1,0:T(8,128)} %bitcast.8), custom_call_target="tpu_custom_call" | custom-call | tf_op jit(solution)/shard_map/unpack/pallas_call | solution.py:375
  (9 shorter events, 0.0 us)
Async XLA Ops:
  14.8 6.2 %collective-permute-start.6 = (f32[24,8,128]{2,1,0:T(8,128)}, f32[24,8,128]{2,1,0:T(8,128)S(1)}, u32[]{:S(2)}, u32[]{:S(2)}) collective-permute-start(f32[24,8,128]{2,1,0:T(8,128)} %get-tuple-element.9.refs_0_), channel_id=1, source_target_pairs={{0,112},{16,0},{32,16},{48,32},{64,48},{80,64},{96,80},{112,96},{1... | collective-permute-start | bytes 294920 | tf_op jit(solution)/shard_map/ppermute | solution.py:390
  14.8 12.7 %collective-permute-start.5 = (f32[24,8,128]{2,1,0:T(8,128)}, f32[24,8,128]{2,1,0:T(8,128)S(1)}, u32[]{:S(2)}, u32[]{:S(2)}) collective-permute-start(f32[24,8,128]{2,1,0:T(8,128)} %get-tuple-element.9.refs_0_), channel_id=1, source_target_pairs={{0,96},{16,112},{32,0},{48,16},{64,32},{80,48},{96,64},{112,80},{1... | collective-permute-start | bytes 294920 | tf_op jit(solution)/shard_map/ppermute | solution.py:390
  15.2 32.5 %collective-permute-start.4 = (f32[24,8,128]{2,1,0:T(8,128)}, f32[24,8,128]{2,1,0:T(8,128)S(1)}, u32[]{:S(2)}, u32[]{:S(2)}) collective-permute-start(f32[24,8,128]{2,1,0:T(8,128)} %get-tuple-element.9.refs_0_), channel_id=1, source_target_pairs={{0,80},{16,96},{32,112},{48,0},{64,16},{80,32},{96,48},{112,64},{1... | collective-permute-start | bytes 294920 | tf_op jit(solution)/shard_map/ppermute | solution.py:390
  15.4 32.3 %collective-permute-start.3 = (f32[24,8,128]{2,1,0:T(8,128)}, f32[24,8,128]{2,1,0:T(8,128)S(1)}, u32[]{:S(2)}, u32[]{:S(2)}) collective-permute-start(f32[24,8,128]{2,1,0:T(8,128)} %get-tuple-element.9.refs_0_), channel_id=1, source_target_pairs={{0,64},{16,80},{32,96},{48,112},{64,0},{80,16},{96,32},{112,48},{1... | collective-permute-start | bytes 294920 | tf_op jit(solution)/shard_map/ppermute | solution.py:390
  18.9 28.9 %collective-permute-start.2 = (f32[24,8,128]{2,1,0:T(8,128)}, f32[24,8,128]{2,1,0:T(8,128)S(1)}, u32[]{:S(2)}, u32[]{:S(2)}) collective-permute-start(f32[24,8,128]{2,1,0:T(8,128)} %get-tuple-element.9.refs_0_), channel_id=1, source_target_pairs={{0,48},{16,64},{32,80},{48,96},{64,112},{80,0},{96,16},{112,32},{1... | collective-permute-start | bytes 294920 | tf_op jit(solution)/shard_map/ppermute | solution.py:390
  21.0 26.7 %copy-start = (f32[24,8,128]{2,1,0:T(8,128)}, f32[24,8,128]{2,1,0:T(8,128)S(1)}, u32[]{:S(2)}) copy-start(f32[24,8,128]{2,1,0:T(8,128)S(1)} %collective-permute-done.6.refs_7_) | copy-start | bytes 294916
  21.0 26.8 %collective-permute-start.1 = (f32[24,8,128]{2,1,0:T(8,128)}, f32[24,8,128]{2,1,0:T(8,128)S(1)}, u32[]{:S(2)}, u32[]{:S(2)}) collective-permute-start(f32[24,8,128]{2,1,0:T(8,128)} %get-tuple-element.9.refs_0_), channel_id=1, source_target_pairs={{0,32},{16,48},{32,64},{48,80},{64,96},{80,112},{96,0},{112,16},{1... | collective-permute-start | bytes 294920 | tf_op jit(solution)/shard_map/ppermute | solution.py:390
  27.5 20.2 %copy-start.1 = (f32[24,8,128]{2,1,0:T(8,128)}, f32[24,8,128]{2,1,0:T(8,128)S(1)}, u32[]{:S(2)}) copy-start(f32[24,8,128]{2,1,0:T(8,128)S(1)} %collective-permute-done.5.refs_6_) | copy-start | bytes 294916
  27.5 20.3 %collective-permute-start = (f32[24,8,128]{2,1,0:T(8,128)}, f32[24,8,128]{2,1,0:T(8,128)S(1)}, u32[]{:S(2)}, u32[]{:S(2)}) collective-permute-start(f32[24,8,128]{2,1,0:T(8,128)} %get-tuple-element.9.refs_0_), channel_id=1, source_target_pairs={{0,16},{16,32},{32,48},{48,64},{64,80},{80,96},{96,112},{112,0},{1... | collective-permute-start | bytes 294920 | tf_op jit(solution)/shard_map/ppermute | solution.py:390
  47.7 0.6 copy-start.2
  47.8 0.6 copy-start.3
  47.8 0.7 copy-start.4
  47.8 0.7 copy-start.5
  47.8 0.7 copy-start.6

commit v2 on v0

v2 whole, which is shorter than its diff:
```python
import jax
import jax.numpy as jnp
from jax import lax
from jax.experimental import pallas as pl
from jax.experimental.pallas import tpu as pltpu
from jax.sharding import PartitionSpec as P

F32 = jnp.float32
POINTS = 64
FIELDS = 2
NSUB = 8
GROUPS = 16
LANES = 128
ROWS = 8
PACK = 5
QB = 8
PB = 8
NEAR = POINTS // GROUPS
SENT = FIELDS * NEAR * 4 + 1
MESSAGE = 2 * PACK + 2
BLOCKS = POINTS // PB


def lane_iota():
    return lax.broadcasted_iota(jnp.int32, (ROWS, LANES), 1)


def row_iota():
    return lax.broadcasted_iota(jnp.int32, (ROWS, LANES), 0)


def pair_wavenumber(slot_ref):
    pair = row_iota() // 2
    m = jnp.full((ROWS, LANES), slot_ref[0], jnp.int32)
    for j in range(1, 4):
        m = jnp.where(pair == j, slot_ref[2 * j], m)
    return m


def down(x):
    return pltpu.roll(x, 1, 0)


def up(x):
    return pltpu.roll(x, ROWS - 1, 0)


def fold(x, m, lane, even, small):
    shift = jnp.where(small, m, m - LANES)
    turn = (lane - shift + LANES) % LANES
    below = lane < shift
    low3 = jnp.where(even, x[2], down(x[3]))
    high3 = jnp.where(even, up(x[2]), x[3])
    high3_t = jnp.take_along_axis(high3, turn, axis=1)
    mix_t = jnp.take_along_axis(x[4], turn, axis=1)
    zero = jnp.where(small, jnp.where(below, high3_t, x[4]), jnp.where(below, mix_t, high3_t))
    one = jnp.where(jnp.logical_and(below, jnp.logical_not(small)), high3_t, x[0])
    last = jnp.full((ROWS, LANES), LANES - 1, jnp.int32)
    spare = jnp.take_along_axis(jnp.where(small, high3_t, mix_t), last, axis=1)
    return (zero, one, x[1], low3), spare


def column(x, k):
    return jnp.take_along_axis(x, jnp.full((ROWS, LANES), k, jnp.int32), axis=1)


def unfold(s, spare, m, lane, even, small):
    shift = jnp.where(small, m, m - LANES)
    back = (lane + shift) % LANES
    after = lane >= LANES - shift
    exact = lane == LANES - 1 - shift
    g0 = jnp.take_along_axis(s[0], back, axis=1)
    g1 = jnp.take_along_axis(s[1], back, axis=1)
    value = jnp.where(after, g0, jnp.where(exact, spare, 0.0))
    high3 = jnp.where(small, value, jnp.where(after, g1, g0))
    high2 = jnp.where(small, 0.0, value)
    low0 = jnp.where(lane >= m, s[0], 0.0)
    low1 = jnp.where(lane + LANES >= m, s[1], 0.0)
    lows = [low0, low1, s[2], s[3]]
    first = [jnp.where(even, low0, 0.0), jnp.where(even, low1, 0.0)]
    first += [jnp.where(even, s[2], down(high2)), jnp.where(even, s[3], down(high3))]
    second = [jnp.where(even, up(low0), 0.0), jnp.where(even, up(low1), 0.0)]
    second += [jnp.where(even, up(s[2]), high2), jnp.where(even, up(s[3]), high3)]
    return first, second


AHEAD = 4
CHUNKS = FIELDS * BLOCKS


def inverse_chunks(inv_hbm, inv_v, sem):
    def copy(i):
        f = i // BLOCKS
        rows = pl.ds(lax.rem(i, BLOCKS) * PB, PB)
        return pltpu.make_async_copy(inv_hbm.at[f, rows], inv_v.at[f, rows], sem.at[i])

    return copy


def next_chunk(copy, i):
    copy(i).wait()

    @pl.when(i + AHEAD < CHUNKS)
    def _():
        copy(i + AHEAD).start()


def start_all(copy, count):
    def step(i, carry):
        copy(i).start()
        return carry

    lax.fori_loop(0, count, step, 0)


def wait_all(copy, count):
    def step(i, carry):
        copy(i).wait()
        return carry

    lax.fori_loop(0, count, step, 0)


def slope_kernel(
    slot_ref, weight_ref, inv_hbm, src_hbm, packed_hbm, msg_hbm, inv_v, src_v, packed_v, e_v, msg_ref, inv_sem, src_sem, out_sem, msg_sem
):
    copy = inverse_chunks(inv_hbm, inv_v, inv_sem)
    sources = [pltpu.make_async_copy(src_hbm.at[f], src_v.at[f], src_sem.at[f]) for f in range(FIELDS)]
    results = [pltpu.make_async_copy(packed_v.at[f], packed_hbm.at[f], out_sem.at[f]) for f in range(FIELDS)]
    sources[0].start()
    start_all(copy, AHEAD)
    m = pair_wavenumber(slot_ref)
    lane = lane_iota()
    even = row_iota() % 2 == 0
    small = m < LANES
    zero = jnp.zeros((ROWS, LANES), F32)
    keep1 = lane + LANES >= m
    keep3 = lane + 3 * LANES >= jnp.where(even, m, 511 - m)
    keep_mix = lane >= jnp.where(small, m, 255 - m)
    for f in range(FIELDS):
        sources[f].wait()

        def pack_point(q, carry):
            s = [[src_v[f, q, c, :, b * LANES:(b + 1) * LANES] for b in range(4)] for c in range(2)]
            first = jnp.where(even, s[0][0], down(s[1][0]))
            late = jnp.where(even, up(s[0][2]), s[1][2])
            packed_v[f, q, 0] = jnp.where(keep1, jnp.where(even, s[0][1], down(s[1][1])), 0.0)
            packed_v[f, q, 1] = jnp.where(even, s[0][2], down(s[1][2]))
            packed_v[f, q, 2] = jnp.where(keep3, s[0][3], 0.0)
            packed_v[f, q, 3] = jnp.where(keep3, s[1][3], 0.0)
            packed_v[f, q, 4] = jnp.where(keep_mix, jnp.where(small, first, late), 0.0)
            return carry

        lax.fori_loop(1, POINTS - 1, pack_point, 0, unroll=2)
        for q in (0, POINTS - 1):
            for v in range(PACK):
                packed_v[f, q, v] = zero
        results[f].start()
        if f + 1 < FIELDS:
            sources[f + 1].start()

        for r in range(2):
            for qb in range(POINTS // ROWS):
                for b in range(4):
                    e_v[r, qb, b] = zero

        def weigh(block, carry):
            next_chunk(copy, f * BLOCKS + block)
            weights = [[weight_ref[0, r, block * PB + p] for p in range(PB)] for r in range(2)]

            def tile_row(qb, carry):
                for b in range(4):
                    low, top = e_v[0, qb, b], e_v[1, qb, b]
                    for p in range(PB):
                        tile = inv_v[f, block * PB + p, qb, :, b * LANES:(b + 1) * LANES]
                        low = low + weights[0][p] * tile
                        top = top + weights[1][p] * tile
                    e_v[0, qb, b] = low
                    e_v[1, qb, b] = top
                return carry

            return lax.fori_loop(0, POINTS // ROWS, tile_row, carry)

        lax.fori_loop(0, BLOCKS, weigh, 0)

        def accumulate(qb, sums):
            sums = list(sums)
            for row in range(ROWS):
                x = [packed_v[f, qb * ROWS + row, v] for v in range(PACK)]
                for r in range(2):
                    e = [jnp.broadcast_to(e_v[r, qb, b, row:row + 1, :], (ROWS, LANES)) for b in range(4)]
                    e = [e[1], e[2], e[3], e[3], jnp.where(small, e[0], e[2])]
                    for v in range(PACK):
                        sums[r * PACK + v] = sums[r * PACK + v] + e[v] * x[v]
            return tuple(sums)

        sums = lax.fori_loop(0, POINTS // ROWS, accumulate, (zero,) * (2 * PACK))
        for i in range(2 * PACK):
            msg_ref[f * MESSAGE + i] = sums[i]
        for r in range(2):
            for b in range(4):
                msg_ref[f * MESSAGE + 2 * PACK + r, 2 * b:2 * b + 1, :] = e_v[r, 0, b, 0:1, :]
                msg_ref[f * MESSAGE + 2 * PACK + r, 2 * b + 1:2 * b + 2, :] = (
                    e_v[r, POINTS // ROWS - 1, b, ROWS - 1:ROWS, :]
                )

    def message_copy(k):
        return pltpu.make_async_copy(msg_ref, msg_hbm.at[k], msg_sem.at[k])

    start_all(message_copy, NSUB)
    for f in range(FIELDS):
        results[f].wait()
    wait_all(message_copy, NSUB)


ANY = pl.BlockSpec(memory_space=pl.ANY)
SCALARS = pl.BlockSpec(memory_space=pltpu.SMEM)
INVERSE_V = pltpu.VMEM((FIELDS, POINTS, POINTS // ROWS, ROWS, 512), F32)
PACKED_V = pltpu.VMEM((FIELDS, POINTS, PACK, ROWS, LANES), F32)
EDGE_V = pltpu.VMEM((FIELDS, POINTS, ROWS, LANES), F32)


def dma(*shape):
    return pltpu.SemaphoreType.DMA(shape)


def slopes(slot, weights, inverse, forcing):
    return pl.pallas_call(
        slope_kernel,
        in_specs=[SCALARS, SCALARS, ANY, ANY],
        out_specs=[ANY, ANY],
        out_shape=[
            jax.ShapeDtypeStruct((FIELDS, POINTS, PACK, ROWS, LANES), F32),
            jax.ShapeDtypeStruct((NSUB, FIELDS * MESSAGE, ROWS, LANES), F32),
        ],
        scratch_shapes=[
            INVERSE_V,
            pltpu.VMEM((FIELDS, POINTS, 2, ROWS, 512), F32),
            pltpu.VMEM((FIELDS, POINTS, PACK, ROWS, LANES), F32),
            pltpu.VMEM((2, POINTS // ROWS, 4, ROWS, LANES), F32),
            pltpu.VMEM((FIELDS * MESSAGE, ROWS, LANES), F32),
            dma(CHUNKS),
            dma(FIELDS),
            dma(FIELDS),
            dma(NSUB),
        ],
        cost_estimate=pl.CostEstimate(flops=20_000_000, bytes_accessed=24_000_000, transcendentals=0),
        name="slopes",
    )(slot, weights, inverse, forcing)


def block_sums(f, inv_v, packed_v, block, small, odd_v):
    zero = jnp.zeros((ROWS, LANES), F32)

    def unit(p, qb, r, b):
        line = inv_v[f, block * PB + p, qb, r:r + 1, b * LANES:(b + 1) * LANES]
        return jnp.broadcast_to(line, (ROWS, LANES))

    def odd_pass(qb, sums):
        sums = list(sums)
        for r in range(ROWS):
            s = [packed_v[f, qb * ROWS + r, v] for v in (0, 2, 3)]
            for p in range(PB):
                one = unit(p, qb, r, 1)
                three = unit(p, qb, r, 3)
                sums[3 * p] = sums[3 * p] + one * s[0]
                sums[3 * p + 1] = sums[3 * p + 1] + three * s[1]
                sums[3 * p + 2] = sums[3 * p + 2] + three * s[2]
        return tuple(sums)

    def even_pass(qb, sums):
        sums = list(sums)
        for r in range(ROWS):
            s = [packed_v[f, qb * ROWS + r, v] for v in (1, 4)]
            for p in range(PB):
                none = unit(p, qb, r, 0)
                two = unit(p, qb, r, 2)
                sums[2 * p] = sums[2 * p] + two * s[0]
                sums[2 * p + 1] = sums[2 * p + 1] + jnp.where(small, none, two) * s[1]
        return tuple(sums)

    odd = lax.fori_loop(0, POINTS // ROWS, odd_pass, (zero,) * (3 * PB))
    for i in range(3 * PB):
        odd_v[i] = odd[i]
    even = lax.fori_loop(0, POINTS // ROWS, even_pass, (zero,) * (2 * PB))
    return [[odd_v[3 * p], even[2 * p], odd_v[3 * p + 1], odd_v[3 * p + 2], even[2 * p + 1]] for p in range(PB)]


def particular_kernel(
    slot_ref, inv_hbm, packed_hbm, part_hbm, edge_hbm, inv_v, packed_v, part_v, edge_v, odd_v, inv_sem, src_sem, part_sem, edge_sem
):
    copy = inverse_chunks(inv_hbm, inv_v, inv_sem)
    sources = [pltpu.make_async_copy(packed_hbm.at[f], packed_v.at[f], src_sem.at[f]) for f in range(FIELDS)]
    sources[0].start()
    start_all(copy, AHEAD)
    small = pair_wavenumber(slot_ref) < LANES

    def part_copy(i):
        f, rows = i // BLOCKS, pl.ds(lax.rem(i, BLOCKS) * PB, PB)
        return pltpu.make_async_copy(part_v.at[f, rows], part_hbm.at[f, rows], part_sem.at[i])

    edges = [pltpu.make_async_copy(edge_v.at[f], edge_hbm.at[f], edge_sem.at[f]) for f in range(FIELDS)]
    for f in range(FIELDS):
        sources[f].wait()
        if f + 1 < FIELDS:
            sources[f + 1].start()

        def step(block, carry):
            next_chunk(copy, f * BLOCKS + block)
            x = block_sums(f, inv_v, packed_v, block, small, odd_v)
            for p in range(PB):
                at = block * PB + p
                for v in range(PACK):
                    part_v[f, at, v] = x[p][v]
                for b in range(4):
                    lanes = slice(b * LANES, (b + 1) * LANES)
                    edge_v[f, at, 2 * b:2 * b + 1, :] = inv_v[f, at, 0, 0:1, lanes]
                    edge_v[f, at, 2 * b + 1:2 * b + 2, :] = inv_v[f, at, POINTS // ROWS - 1, ROWS - 1:ROWS, lanes]
            part_copy(f * BLOCKS + block).start()
            return carry

        lax.fori_loop(0, BLOCKS, step, 0)
        edges[f].start()
    wait_all(part_copy, CHUNKS)
    for edge in edges:
        edge.wait()


def particular(slot, inverse, packed):
    return pl.pallas_call(
        particular_kernel,
        in_specs=[SCALARS, ANY, ANY],
        out_specs=[ANY, ANY],
        out_shape=[
            jax.ShapeDtypeStruct((FIELDS, POINTS, PACK, ROWS, LANES), F32),
            jax.ShapeDtypeStruct((FIELDS, POINTS, ROWS, LANES), F32),
        ],
        scratch_shapes=[
            INVERSE_V,
            PACKED_V,
            PACKED_V,
            EDGE_V,
            pltpu.VMEM((3 * PB, ROWS, LANES), F32),
            dma(CHUNKS),
            dma(FIELDS),
            dma(CHUNKS),
            dma(FIELDS),
        ],
        cost_estimate=pl.CostEstimate(flops=90_000_000, bytes_accessed=24_000_000, transcendentals=0),
        name="particular",
    )(slot, inverse, packed)


def solve_interface(f, all_v, u_v, small):
    base = f * MESSAGE
    zero = jnp.zeros((ROWS, LANES), F32)
    for v in range(PACK):
        u_v[0, f, v] = zero
        u_v[NSUB, f, v] = zero

    def coefficient(t, r, k, b):
        return all_v[t, base + 2 * PACK + r, pl.ds(2 * b + k, ROWS, stride=0), :]

    ratio = [zero] * PACK
    reduced = [zero] * PACK
    ratios = []
    reduceds = []
    for level in range(NSUB - 1):
        factors = []
        for b in range(4):
            lower = coefficient(level, 1, 0, b)
            middle = coefficient(level, 1, 1, b) - coefficient(level + 1, 0, 0, b)
            upper = -coefficient(level + 1, 0, 1, b)
            factors.append((lower, middle, upper))
        mixed = tuple(jnp.where(small, x, y) for x, y in zip(factors[0], factors[2]))
        new_ratio, new_reduced = [None] * PACK, [None] * PACK
        for v, (lower, middle, upper) in enumerate((factors[1], factors[2], factors[3], factors[3], mixed)):
            right = all_v[level + 1, base + v] - all_v[level, base + PACK + v]
            inverted = last if v == 3 else 1.0 / (middle - lower * ratio[v])
            last = inverted
            new_ratio[v] = upper * inverted
            new_reduced[v] = (right - lower * reduced[v]) * inverted
        ratio, reduced = new_ratio, new_reduced
        ratios.append(ratio)
        reduceds.append(reduced)
    later = [zero] * PACK
    for level in range(NSUB - 2, -1, -1):
        later = [reduceds[level][v] - ratios[level][v] * later[v] for v in range(PACK)]
        for v in range(PACK):
            u_v[level + 1, f, v] = later[v]


PER = PB // NEAR


def pack_kernel(
    slot_ref, all_hbm, part_hbm, edge_hbm, out_hbm, all_v, u_v, part_v, edge_v, out_v, all_sem, part_sem, edge_sem, out_sem
):
    messages = pltpu.make_async_copy(all_hbm, all_v, all_sem)
    messages.start()
    edges = pltpu.make_async_copy(edge_hbm, edge_v, edge_sem)
    edges.start()

    def part_copy(i):
        rows = pl.ds(i * PB, PB)
        return pltpu.make_async_copy(part_hbm.at[:, rows], part_v.at[:, rows], part_sem.at[i])

    start_all(part_copy, BLOCKS)
    m = pair_wavenumber(slot_ref)
    lane = lane_iota()
    even = row_iota() % 2 == 0
    small = m < LANES
    messages.wait()
    for f in range(FIELDS):
        solve_interface(f, all_v, u_v, small)
    edges.wait()
    sub = lax.axis_index("sub")

    def out_copy(i):
        rows = pl.ds(i * PER, PER)
        return pltpu.make_async_copy(out_v.at[rows], out_hbm.at[rows], out_sem.at[i])

    def step(block, carry):
        part_copy(block).wait()
        for d in range(PER):
            dest = block * PER + d
            extra = jnp.where(lane == FIELDS * NEAR, m.astype(F32), 0.0)
            for f in range(FIELDS):
                u_low = [u_v[sub, f, v] for v in range(PACK)]
                u_top = [u_v[sub + 1, f, v] for v in range(PACK)]
                for k in range(NEAR):
                    p = block * PB + d * NEAR + k
                    low = [edge_v[f, p, pl.ds(2 * b, ROWS, stride=0), :] for b in range(4)]
                    top = [edge_v[f, p, pl.ds(2 * b + 1, ROWS, stride=0), :] for b in range(4)]
                    low = [low[1], low[2], low[3], low[3], jnp.where(small, low[0], low[2])]
                    top = [top[1], top[2], top[3], top[3], jnp.where(small, top[0], top[2])]
                    x = [part_v[f, p, v] + u_low[v] * low[v] + u_top[v] * top[v] for v in range(PACK)]
                    s, spare = fold(x, m, lane, even, small)
                    at = f * NEAR + k
                    for b in range(4):
                        out_v[dest, at * 4 + b] = s[b]
                    extra = jnp.where(lane == at, spare, extra)
            out_v[dest, SENT - 1] = extra
        out_copy(block).start()
        return carry

    lax.fori_loop(0, BLOCKS, step, 0)
    wait_all(out_copy, BLOCKS)


SENT_V = pltpu.VMEM((GROUPS, SENT, ROWS, LANES), F32)


def pack(slot, messages, part, edges):
    return pl.pallas_call(
        pack_kernel,
        in_specs=[SCALARS, ANY, ANY, ANY],
        out_specs=ANY,
        out_shape=jax.ShapeDtypeStruct((GROUPS, SENT, ROWS, LANES), F32),
        scratch_shapes=[
            pltpu.VMEM((NSUB, FIELDS * MESSAGE, ROWS, LANES), F32),
            pltpu.VMEM((NSUB + 1, FIELDS, PACK, ROWS, LANES), F32),
            PACKED_V,
            EDGE_V,
            SENT_V,
            pltpu.SemaphoreType.DMA,
            dma(BLOCKS),
            pltpu.SemaphoreType.DMA,
            dma(BLOCKS),
        ],
        name="pack",
    )(slot, messages, part, edges)


STEPS = 8
FROM = GROUPS // STEPS


def unpack_kernel(in_hbm, out_hbm, in_v, out_v, in_sem, out_sem):
    def in_copy(i):
        rows = pl.ds(i * FROM, FROM)
        return pltpu.make_async_copy(in_hbm.at[rows], in_v.at[rows], in_sem.at[i])

    def out_copy(i):
        rows = pl.ds(pl.multiple_of(i * FROM * ROWS, ROWS), FROM * ROWS)
        return pltpu.make_async_copy(out_v.at[:, :, :, rows, :], out_hbm.at[:, :, :, rows, :], out_sem.at[i])

    start_all(in_copy, STEPS)
    lane = lane_iota()
    even = row_iota() % 2 == 0

    def step(i, carry):
        in_copy(i).wait()
        for d in range(FROM):
            g = i * FROM + d
            extras = in_v[g, SENT - 1]
            m = column(extras, FIELDS * NEAR).astype(jnp.int32)
            small = m < LANES
            rows = pl.ds(pl.multiple_of(g * ROWS, ROWS), ROWS)
            for f in range(FIELDS):
                for k in range(NEAR):
                    at = f * NEAR + k
                    s = [in_v[g, at * 4 + b] for b in range(4)]
                    tiles = unfold(s, column(extras, at), m, lane, even, small)
                    for c in range(2):
                        for b in range(4):
                            out_v[f, k, c, rows, b * LANES:(b + 1) * LANES] = tiles[c][b]
        out_copy(i).start()
        return carry

    lax.fori_loop(0, STEPS, step, 0)
    wait_all(out_copy, STEPS)


def unpack(received):
    return pl.pallas_call(
        unpack_kernel,
        in_specs=[ANY],
        out_specs=ANY,
        out_shape=jax.ShapeDtypeStruct((FIELDS, NEAR, 2, GROUPS * ROWS, 512), F32),
        scratch_shapes=[
            SENT_V,
            pltpu.VMEM((FIELDS, NEAR, 2, GROUPS * ROWS, 512), F32),
            dma(STEPS),
            dma(STEPS),
        ],
        name="unpack",
    )(received)


def over_ma(sent):
    flat = sent.reshape(GROUPS, SENT * ROWS, LANES)
    received = lax.all_to_all(flat, "ma", split_axis=0, concat_axis=0, tiled=True)
    return received.reshape(GROUPS, SENT, ROWS, LANES)


def body(forcing, slot_wavenumber, inverse, edge_weights):
    inverse = inverse.reshape(FIELDS, POINTS, POINTS // ROWS, ROWS, 512)
    packed, messages = slopes(slot_wavenumber, edge_weights, inverse, forcing)
    messages = lax.all_to_all(messages, "sub", split_axis=0, concat_axis=0, tiled=True)
    part, edges = particular(slot_wavenumber, inverse, packed)
    sent = pack(slot_wavenumber, messages, part, edges)
    return unpack(over_ma(sent))


def solution(mesh):
    return jax.shard_map(
        body,
        mesh=mesh,
        in_specs=(
            P(None, "sub", None, "ma", None),
            P("ma"),
            P("sub", None, None, None, None),
            P("sub", None, None),
        ),
        out_specs=P(None, ("sub", "ma"), None, None, None),
        check_vma=False,
    )
```

time: 235 us -> 80.4 us (0.34)
  matrix products: 70.3 us -> 0 us
  local copies, waits for them, and re-layouts: 68.2 us -> 0.88 us
  Pallas kernels: 0 us -> 36.5 us
  blocking collectives: 56.5 us -> 35.8 us
  waiting for transfers between devices: 15.9 us -> 0.01 us
  other arithmetic: 14.9 us -> 0 us
    dot_general x7 -> x0, matrix products: 70.3 us -> none  [the longest x1 57.6 us: body(): jnp.einsum('fpql,fqcml->fpcml', block_inverse, source, precision=HIGH)]
    pallas_call x0 -> x4, Pallas kernels: none -> 36.5 us  [the longest x1 17.8 us: particular(): pl.pallas_call(particular_kernel, in_specs=[SCALARS, ANY, ANY], out_specs...]
    squeeze x1 -> x0, local copies, waits for them, and re-layouts: 30.5 us -> none  [body(): block_inverse = inverse[0]]
    all_to_all x1, blocking collectives: 56.5 us -> 35.8 us  [over_ma(): lax.all_to_all(flat, 'ma', split_axis=0, concat_axis=0, tiled=True)]
    all_to_all x1, waiting for transfers between devices: 15.9 us -> 0.01 us  [body(): lax.all_to_all(messages, 'sub', split_axis=0, concat_axis=0, tiled=True)]
    mul x11 -> x0, local copies, waits for them, and re-layouts: 9.8 us -> none  [the longest x1 8.66 us: body(): forcing * kept_modes[None, None, None, :, :]]
    add x1 -> x0, other arithmetic: 8.58 us -> none  [body(): solution = solution + upper_value[:, None] * upper_unit[:, :, None, None, :]]
    dot_general x7 -> x0, local copies, waits for them, and re-layouts: 7.74 us -> none  [the longest x2 7.68 us: body(): jnp.einsum('p,fpcml->fcml', edge_rows[1], particular, precision=HIGH)]
  transfers between devices with their start and end apart: 1 -> 1, of which waited for: 1 -> 0; matrix products, arithmetic and copies ran while one was open for 0% -> 0% of each run, Pallas kernels for 0% -> 22%
where the time goes in v2:
time: 80.4 us; the launch traced here: 80.1 us
  Pallas kernels  36.5 us (45%)
  blocking collectives  35.8 us (45%)
  starting transfers between devices  6.81 us (8%)
  local copies, waits for them, and re-layouts  0.88 us (1%)
    all_to_all x1, blocking collectives, over_ma(): lax.all_to_all(flat, 'ma', split_axis=0, concat_axis=0, tiled=True)  35.8 us
    pallas_call x1, Pallas kernels, particular(): pl.pallas_call(particular_kernel, in_specs=[SCALARS, ANY, ANY], out_specs...  17.8 us
    pallas_call x1, Pallas kernels, slopes(): pl.pallas_call(slope_kernel, in_specs=[SCALARS, SCALARS, ANY, ANY], out_s...  10.8 us
    all_to_all x1, starting transfers between devices, body(): lax.all_to_all(messages, 'sub', split_axis=0, concat_axis=0, tiled=True)  6.81 us
    pallas_call x1, Pallas kernels, pack(): pl.pallas_call(pack_kernel, in_specs=[SCALARS, ANY, ANY, ANY], out_specs=...  4.43 us
    pallas_call x1, Pallas kernels, unpack(): pl.pallas_call(unpack_kernel, in_specs=[ANY], out_specs=ANY, out_shape=ja...  3.52 us
  transfers between devices with their start and end apart: 1, of which 0 were waited for; matrix products, arithmetic and copies ran while one was open for 0% of the time, Pallas kernels for 22%

profile of v2, /device:TPU:1, one launch (start us, length us, event | category | flops | bytes accessed | tf_op | source)
XLA Modules:
  0.0 80.1 jit_solution(14736028091020085839)
XLA Ops:
  0.0 10.8 %slopes.1 = (f32[2,64,5,8,128]{4,3,2,1,0:T(8,128)}, f32[8,24,8,128]{3,2,1,0:T(8,128)}) custom-call(s32[8]{0:T(128)} %slot_ref.5, f32[1,2,64]{2,1,0:T(2,128)} %weight_ref.1, f32[2,64,8,8,512]{4,3,2,1,0:T(8,128)} %bitcast.3, f32[2,64,2,8,512]{4,3,2,1,0:T(8,128)} %src_hbm.1), custom_call_target="tpu_custom_call" | custom-call | flops 20000000 | bytes 24000000 | tf_op jit(solution)/shard_map/slopes/pallas_call | solution.py:228
  10.8 6.8 %all-to-all-start = ((f32[8,24,8,128]{3,2,1,0:T(8,128)}), f32[8,24,8,128]{3,2,1,0:T(8,128)S(1)}, u32[]{:S(2)}, u32[]{:S(2)}) async-start(f32[8,24,8,128]{3,2,1,0:T(8,128)} %get-tuple-element.9), calls=%async_computation | async-start | bytes 1572864 | tf_op jit(solution)/shard_map/all_to_all | solution.py:540
  17.6 17.8 %particular.1 = (f32[2,64,5,8,128]{4,3,2,1,0:T(8,128)}, f32[2,64,8,128]{3,2,1,0:T(8,128)}) custom-call(s32[8]{0:T(128)} %slot_ref.5, f32[2,64,8,8,512]{4,3,2,1,0:T(8,128)} %bitcast.4, f32[2,64,5,8,128]{4,3,2,1,0:T(8,128)} %get-tuple-element.10.packed_hbm), custom_call_target="tpu_custom_call" | custom-call | flops 90000000 | bytes 24000000 | tf_op jit(solution)/shard_map/particular/pallas_call | solution.py:330
  35.4 0.0 all-to-all-done.all_hbm
  35.4 0.0 copy-start
  35.4 0.9 %copy-done = f32[8,24,8,128]{3,2,1,0:T(8,128)} copy-done((f32[8,24,8,128]{3,2,1,0:T(8,128)}, f32[8,24,8,128]{3,2,1,0:T(8,128)S(1)}, u32[]{:S(2)}) %copy-start) | copy-done | bytes 786456
  36.3 4.4 %pack.1 = f32[16,33,8,128]{3,2,1,0:T(8,128)} custom-call(s32[8]{0:T(128)} %slot_ref.5, f32[8,24,8,128]{3,2,1,0:T(8,128)} %copy-done, f32[2,64,5,8,128]{4,3,2,1,0:T(8,128)} %get-tuple-element.11.part_hbm, f32[2,64,8,128]{3,2,1,0:T(8,128)} %get-tuple-element.12.edge_hbm), custom_call_target="tpu_custom_call" | custom-call | tf_op jit(solution)/shard_map/pack/pallas_call | solution.py:455
  40.8 35.8 %all_to_all.10 = f32[16,264,128]{2,1,0:T(8,128)} all-to-all(f32[16,264,128]{2,1,0:T(8,128)} %bitcast.5), channel_id=1, replica_groups=mesh['sub'=8,'ma'=16] {'ma'}, dimensions={0} | all-to-all | bytes 4325376 | tf_op jit(solution)/shard_map/all_to_all | solution.py:533
  76.6 3.5 %unpack.1 = f32[2,4,2,128,512]{4,3,2,1,0:T(8,128)} custom-call(f32[16,33,8,128]{3,2,1,0:T(8,128)} %bitcast.6), custom_call_target="tpu_custom_call" | custom-call | tf_op jit(solution)/shard_map/unpack/pallas_call | solution.py:516
Async XLA Ops:
  10.8 24.6 %all-to-all-start = ((f32[8,24,8,128]{3,2,1,0:T(8,128)}), f32[8,24,8,128]{3,2,1,0:T(8,128)S(1)}, u32[]{:S(2)}, u32[]{:S(2)}) async-start(f32[8,24,8,128]{3,2,1,0:T(8,128)} %get-tuple-element.9), calls=%async_computation | async-start | bytes 1572864 | tf_op jit(solution)/shard_map/all_to_all | solution.py:540
  35.4 0.9 %copy-start = (f32[8,24,8,128]{3,2,1,0:T(8,128)}, f32[8,24,8,128]{3,2,1,0:T(8,128)S(1)}, u32[]{:S(2)}) copy-start(f32[8,24,8,128]{3,2,1,0:T(8,128)S(1)} %all-to-all-done.all_hbm) | copy-start | bytes 2359300

commit v3 on v2

--- a/solution.py
+++ b/solution.py
@@ -84,7 +84,8 @@
     return first, second
 
 
-AHEAD = 4
+AHEAD = 8
+EARLY = 3
 CHUNKS = FIELDS * BLOCKS
 
 
@@ -105,28 +106,34 @@
         copy(i + AHEAD).start()
 
 
-def start_all(copy, count):
+def start_all(copy, count, first=0):
     def step(i, carry):
         copy(i).start()
         return carry
 
-    lax.fori_loop(0, count, step, 0)
-
-
-def wait_all(copy, count):
+    lax.fori_loop(first, first + count, step, 0)
+
+
+def wait_all(copy, count, first=0):
     def step(i, carry):
         copy(i).wait()
         return carry
 
-    lax.fori_loop(0, count, step, 0)
+    lax.fori_loop(first, count, step, 0)
 
 
 def slope_kernel(
-    slot_ref, weight_ref, inv_hbm, src_hbm, packed_hbm, msg_hbm, inv_v, src_v, packed_v, e_v, msg_ref, inv_sem, src_sem, out_sem, msg_sem
+    slot_ref, weight_ref, inv_hbm, src_hbm, packed_hbm, msg_hbm, part_hbm, edge_hbm,
+    inv_v, src_v, packed_v, e_v, msg_ref, part_v, edge_v, odd_v, inv_sem, src_sem, out_sem, msg_sem, early_sem
 ):
     copy = inverse_chunks(inv_hbm, inv_v, inv_sem)
     sources = [pltpu.make_async_copy(src_hbm.at[f], src_v.at[f], src_sem.at[f]) for f in range(FIELDS)]
     results = [pltpu.make_async_copy(packed_v.at[f], packed_hbm.at[f], out_sem.at[f]) for f in range(FIELDS)]
+    rows = pl.ds(0, EARLY * PB)
+    early = [
+        pltpu.make_async_copy(part_v.at[0, rows], part_hbm, early_sem.at[0]),
+        pltpu.make_async_copy(edge_v.at[0, rows], edge_hbm, early_sem.at[1]),
+    ]
     sources[0].start()
     start_all(copy, AHEAD)
     m = pair_wavenumber(slot_ref)
@@ -140,7 +147,12 @@
     for f in range(FIELDS):
         sources[f].wait()
 
-        def pack_point(q, carry):
+        def pack_points(i, carry):
+            for k in range(8):
+                pack_point(i * 8 + k)
+            return carry
+
+        def pack_point(q):
             s = [[src_v[f, q, c, :, b * LANES:(b + 1) * LANES] for b in range(4)] for c in range(2)]
             first = jnp.where(even, s[0][0], down(s[1][0]))
             late = jnp.where(even, up(s[0][2]), s[1][2])
@@ -149,9 +161,8 @@
             packed_v[f, q, 2] = jnp.where(keep3, s[0][3], 0.0)
             packed_v[f, q, 3] = jnp.where(keep3, s[1][3], 0.0)
             packed_v[f, q, 4] = jnp.where(keep_mix, jnp.where(small, first, late), 0.0)
-            return carry
-
-        lax.fori_loop(1, POINTS - 1, pack_point, 0, unroll=2)
+
+        lax.fori_loop(0, POINTS // 8, pack_points, 0)
         for q in (0, POINTS - 1):
             for v in range(PACK):
                 packed_v[f, q, v] = zero
@@ -179,9 +190,20 @@
                     e_v[1, qb, b] = top
                 return carry
 
-            return lax.fori_loop(0, POINTS // ROWS, tile_row, carry)
-
-        lax.fori_loop(0, BLOCKS, weigh, 0)
+            return lax.fori_loop(0, POINTS // ROWS, tile_row, carry, unroll=2)
+
+        def weigh_and_solve(block, carry):
+            weigh(block, carry)
+            solve_block(f, inv_v, packed_v, block, small, odd_v, part_v, edge_v)
+            return carry
+
+        if f == 0:
+            lax.fori_loop(0, EARLY, weigh_and_solve, 0)
+            for copy_out in early:
+                copy_out.start()
+            lax.fori_loop(EARLY, BLOCKS, weigh, 0)
+        else:
+            lax.fori_loop(0, BLOCKS, weigh, 0)
 
         def accumulate(qb, sums):
             sums = list(sums)
@@ -208,8 +230,8 @@
         return pltpu.make_async_copy(msg_ref, msg_hbm.at[k], msg_sem.at[k])
 
     start_all(message_copy, NSUB)
-    for f in range(FIELDS):
-        results[f].wait()
+    for copy_out in results + early:
+        copy_out.wait()
     wait_all(message_copy, NSUB)
 
 
@@ -228,10 +250,12 @@
     return pl.pallas_call(
         slope_kernel,
         in_specs=[SCALARS, SCALARS, ANY, ANY],
-        out_specs=[ANY, ANY],
+        out_specs=[ANY] * 4,
         out_shape=[
             jax.ShapeDtypeStruct((FIELDS, POINTS, PACK, ROWS, LANES), F32),
             jax.ShapeDtypeStruct((NSUB, FIELDS * MESSAGE, ROWS, LANES), F32),
+            jax.ShapeDtypeStruct((EARLY * PB, PACK, ROWS, LANES), F32),
+            jax.ShapeDtypeStruct((EARLY * PB, ROWS, LANES), F32),
         ],
         scratch_shapes=[
             INVERSE_V,
@@ -239,10 +263,14 @@
             pltpu.VMEM((FIELDS, POINTS, PACK, ROWS, LANES), F32),
             pltpu.VMEM((2, POINTS // ROWS, 4, ROWS, LANES), F32),
             pltpu.VMEM((FIELDS * MESSAGE, ROWS, LANES), F32),
+            pltpu.VMEM((1, EARLY * PB, PACK, ROWS, LANES), F32),
+            pltpu.VMEM((1, EARLY * PB, ROWS, LANES), F32),
+            pltpu.VMEM((3 * PB, ROWS, LANES), F32),
             dma(CHUNKS),
             dma(FIELDS),
             dma(FIELDS),
             dma(NSUB),
+            dma(2),
         ],
         cost_estimate=pl.CostEstimate(flops=20_000_000, bytes_accessed=24_000_000, transcendentals=0),
         name="slopes",
@@ -256,9 +284,9 @@
         line = inv_v[f, block * PB + p, qb, r:r + 1, b * LANES:(b + 1) * LANES]
         return jnp.broadcast_to(line, (ROWS, LANES))
 
-    def odd_pass(qb, sums):
+    def odd_rows(qb, sums, rows):
         sums = list(sums)
-        for r in range(ROWS):
+        for r in rows:
             s = [packed_v[f, qb * ROWS + r, v] for v in (0, 2, 3)]
             for p in range(PB):
                 one = unit(p, qb, r, 1)
@@ -268,9 +296,9 @@
                 sums[3 * p + 2] = sums[3 * p + 2] + three * s[2]
         return tuple(sums)
 
-    def even_pass(qb, sums):
+    def even_rows(qb, sums, rows):
         sums = list(sums)
-        for r in range(ROWS):
+        for r in rows:
             s = [packed_v[f, qb * ROWS + r, v] for v in (1, 4)]
             for p in range(PB):
                 none = unit(p, qb, r, 0)
@@ -279,11 +307,29 @@
                 sums[2 * p + 1] = sums[2 * p + 1] + jnp.where(small, none, two) * s[1]
         return tuple(sums)
 
-    odd = lax.fori_loop(0, POINTS // ROWS, odd_pass, (zero,) * (3 * PB))
+    def all_rows(rows_of, sums):
+        last = POINTS // ROWS - 1
+        sums = rows_of(0, sums, range(1, ROWS))
+        sums = lax.fori_loop(1, last, lambda qb, c: rows_of(qb, c, range(ROWS)), sums)
+        return rows_of(last, sums, range(ROWS - 1))
+
+    odd = all_rows(odd_rows, (zero,) * (3 * PB))
     for i in range(3 * PB):
         odd_v[i] = odd[i]
-    even = lax.fori_loop(0, POINTS // ROWS, even_pass, (zero,) * (2 * PB))
+    even = all_rows(even_rows, (zero,) * (2 * PB))
     return [[odd_v[3 * p], even[2 * p], odd_v[3 * p + 1], odd_v[3 * p + 2], even[2 * p + 1]] for p in range(PB)]
+
+
+def solve_block(f, inv_v, packed_v, block, small, odd_v, part_v, edge_v):
+    x = block_sums(f, inv_v, packed_v, block, small, odd_v)
+    for p in range(PB):
+        at = block * PB + p
+        for v in range(PACK):
+            part_v[f, at, v] = x[p][v]
+        for b in range(4):
+            lanes = slice(b * LANES, (b + 1) * LANES)
+            edge_v[f, at, 2 * b:2 * b + 1, :] = inv_v[f, at, 0, 0:1, lanes]
+            edge_v[f, at, 2 * b + 1:2 * b + 2, :] = inv_v[f, at, POINTS // ROWS - 1, ROWS - 1:ROWS, lanes]
 
 
 def particular_kernel(
@@ -292,14 +338,17 @@
     copy = inverse_chunks(inv_hbm, inv_v, inv_sem)
     sources = [pltpu.make_async_copy(packed_hbm.at[f], packed_v.at[f], src_sem.at[f]) for f in range(FIELDS)]
     sources[0].start()
-    start_all(copy, AHEAD)
+    start_all(copy, AHEAD, EARLY)
     small = pair_wavenumber(slot_ref) < LANES
 
     def part_copy(i):
         f, rows = i // BLOCKS, pl.ds(lax.rem(i, BLOCKS) * PB, PB)
         return pltpu.make_async_copy(part_v.at[f, rows], part_hbm.at[f, rows], part_sem.at[i])
 
-    edges = [pltpu.make_async_copy(edge_v.at[f], edge_hbm.at[f], edge_sem.at[f]) for f in range(FIELDS)]
+    edges = []
+    for f in range(FIELDS):
+        late = pl.ds(EARLY * PB if f == 0 else 0, POINTS - (EARLY * PB if f == 0 else 0))
+        edges.append(pltpu.make_async_copy(edge_v.at[f, late], edge_hbm.at[f, late], edge_sem.at[f]))
     for f in range(FIELDS):
         sources[f].wait()
         if f + 1 < FIELDS:
@@ -307,21 +356,13 @@
 
         def step(block, carry):
             next_chunk(copy, f * BLOCKS + block)
-            x = block_sums(f, inv_v, packed_v, block, small, odd_v)
-            for p in range(PB):
-                at = block * PB + p
-                for v in range(PACK):
-                    part_v[f, at, v] = x[p][v]
-                for b in range(4):
-                    lanes = slice(b * LANES, (b + 1) * LANES)
-                    edge_v[f, at, 2 * b:2 * b + 1, :] = inv_v[f, at, 0, 0:1, lanes]
-                    edge_v[f, at, 2 * b + 1:2 * b + 2, :] = inv_v[f, at, POINTS // ROWS - 1, ROWS - 1:ROWS, lanes]
+            solve_block(f, inv_v, packed_v, block, small, odd_v, part_v, edge_v)
             part_copy(f * BLOCKS + block).start()
             return carry
 
-        lax.fori_loop(0, BLOCKS, step, 0)
+        lax.fori_loop(EARLY if f == 0 else 0, BLOCKS, step, 0)
         edges[f].start()
-    wait_all(part_copy, CHUNKS)
+    wait_all(part_copy, CHUNKS, EARLY)
     for edge in edges:
         edge.wait()
 
@@ -394,18 +435,37 @@
 
 
 def pack_kernel(
-    slot_ref, all_hbm, part_hbm, edge_hbm, out_hbm, all_v, u_v, part_v, edge_v, out_v, all_sem, part_sem, edge_sem, out_sem
+    slot_ref, all_hbm, early_part, early_edge, part_hbm, edge_hbm, out_hbm,
+    all_v, u_v, part_v, edge_v, out_v, all_sem, part_sem, edge_sem, early_sem, out_sem
 ):
     messages = pltpu.make_async_copy(all_hbm, all_v, all_sem)
     messages.start()
-    edges = pltpu.make_async_copy(edge_hbm, edge_v, edge_sem)
-    edges.start()
+    rows = pl.ds(0, EARLY * PB)
+    late = pl.ds(EARLY * PB, POINTS - EARLY * PB)
+    edges = [
+        pltpu.make_async_copy(early_edge, edge_v.at[0, rows], edge_sem.at[0]),
+        pltpu.make_async_copy(edge_hbm.at[0, late], edge_v.at[0, late], edge_sem.at[1]),
+        pltpu.make_async_copy(edge_hbm.at[1], edge_v.at[1], edge_sem.at[2]),
+    ]
+    for edge in edges:
+        edge.start()
+
+    def first_copy(i):
+        rows = pl.ds(i * PB, PB)
+        return pltpu.make_async_copy(early_part.at[rows], part_v.at[0, rows], early_sem.at[i])
+
+    def late_copy(i):
+        rows = pl.ds(i * PB, PB)
+        return pltpu.make_async_copy(part_hbm.at[0, rows], part_v.at[0, rows], early_sem.at[i])
 
     def part_copy(i):
         rows = pl.ds(i * PB, PB)
-        return pltpu.make_async_copy(part_hbm.at[:, rows], part_v.at[:, rows], part_sem.at[i])
-
-    start_all(part_copy, BLOCKS)
+        return pltpu.make_async_copy(part_hbm.at[1, rows], part_v.at[1, rows], part_sem.at[i])
+
+    start_all(first_copy, EARLY)
+    start_all(part_copy, EARLY)
+    start_all(late_copy, BLOCKS - EARLY, EARLY)
+    start_all(part_copy, BLOCKS - EARLY, EARLY)
     m = pair_wavenumber(slot_ref)
     lane = lane_iota()
     even = row_iota() % 2 == 0
@@ -413,7 +473,8 @@
     messages.wait()
     for f in range(FIELDS):
         solve_interface(f, all_v, u_v, small)
-    edges.wait()
+    for edge in edges:
+        edge.wait()
     sub = lax.axis_index("sub")
 
     def out_copy(i):
@@ -421,6 +482,7 @@
         return pltpu.make_async_copy(out_v.at[rows], out_hbm.at[rows], out_sem.at[i])
 
     def step(block, carry):
+        late_copy(block).wait()
         part_copy(block).wait()
         for d in range(PER):
             dest = block * PER + d
@@ -451,10 +513,10 @@
 SENT_V = pltpu.VMEM((GROUPS, SENT, ROWS, LANES), F32)
 
 
-def pack(slot, messages, part, edges):
+def pack(slot, messages, early_part, early_edge, part, edges):
     return pl.pallas_call(
         pack_kernel,
-        in_specs=[SCALARS, ANY, ANY, ANY],
+        in_specs=[SCALARS] + [ANY] * 5,
         out_specs=ANY,
         out_shape=jax.ShapeDtypeStruct((GROUPS, SENT, ROWS, LANES), F32),
         scratch_shapes=[
@@ -465,11 +527,12 @@
             SENT_V,
             pltpu.SemaphoreType.DMA,
             dma(BLOCKS),
-            pltpu.SemaphoreType.DMA,
+            dma(3),
+            dma(BLOCKS),
             dma(BLOCKS),
         ],
         name="pack",
-    )(slot, messages, part, edges)
+    )(slot, messages, early_part, early_edge, part, edges)
 
 
 STEPS = 8
@@ -536,10 +599,10 @@
 
 def body(forcing, slot_wavenumber, inverse, edge_weights):
     inverse = inverse.reshape(FIELDS, POINTS, POINTS // ROWS, ROWS, 512)
-    packed, messages = slopes(slot_wavenumber, edge_weights, inverse, forcing)
+    packed, messages, early_part, early_edge = slopes(slot_wavenumber, edge_weights, inverse, forcing)
     messages = lax.all_to_all(messages, "sub", split_axis=0, concat_axis=0, tiled=True)
     part, edges = particular(slot_wavenumber, inverse, packed)
-    sent = pack(slot_wavenumber, messages, part, edges)
+    sent = pack(slot_wavenumber, messages, early_part, early_edge, part, edges)
     return unpack(over_ma(sent))
 
 

time: 80.4 us -> 77 us (0.958)
  Pallas kernels: 36.5 us -> 33.2 us
    pallas_call x1, Pallas kernels: 17.8 us -> 14.4 us  [particular(): pl.pallas_call(particular_kernel, in_specs=[SCALARS, ANY, ANY], out_specs...]
  transfers between devices with their start and end apart: 1 -> 1, of which waited for: 0 -> 0; matrix products, arithmetic and copies ran while one was open for 0% -> 0% of each run, Pallas kernels for 22% -> 19%
where the time goes in v3:
time: 77 us; the launch traced here: 76.8 us
  blocking collectives  35.8 us (46%)
  Pallas kernels  33.2 us (43%)
  starting transfers between devices  6.81 us (9%)
  local copies, waits for them, and re-layouts  0.88 us (1%)
    all_to_all x1, blocking collectives, over_ma(): lax.all_to_all(flat, 'ma', split_axis=0, concat_axis=0, tiled=True)  35.8 us
    pallas_call x1, Pallas kernels, particular(): pl.pallas_call(particular_kernel, in_specs=[SCALARS, ANY, ANY], out_specs...  14.4 us
    pallas_call x1, Pallas kernels, slopes(): pl.pallas_call(slope_kernel, in_specs=[SCALARS, SCALARS, ANY, ANY], out_s...  10.5 us
    all_to_all x1, starting transfers between devices, body(): lax.all_to_all(messages, 'sub', split_axis=0, concat_axis=0, tiled=True)  6.81 us
    pallas_call x1, Pallas kernels, pack(): pl.pallas_call(pack_kernel, in_specs=[SCALARS] + [ANY] * 5, out_specs=ANY...  4.68 us
    pallas_call x1, Pallas kernels, unpack(): pl.pallas_call(unpack_kernel, in_specs=[ANY], out_specs=ANY, out_shape=ja...  3.52 us
  transfers between devices with their start and end apart: 1, of which 0 were waited for; matrix products, arithmetic and copies ran while one was open for 0% of the time, Pallas kernels for 19%

profile of v3, /device:TPU:1, one launch (start us, length us, event | category | flops | bytes accessed | tf_op | source)
XLA Modules:
  0.0 76.8 jit_solution(13591400477874656320)
XLA Ops:
  0.0 10.5 %slopes.1 = (f32[2,64,5,8,128]{4,3,2,1,0:T(8,128)}, f32[8,24,8,128]{3,2,1,0:T(8,128)}, f32[24,5,8,128]{3,2,1,0:T(8,128)}, f32[24,8,128]{2,1,0:T(8,128)}) custom-call(s32[8]{0:T(128)} %slot_ref.5, f32[1,2,64]{2,1,0:T(2,128)} %weight_ref.1, f32[2,64,8,8,512]{4,3,2,1,0:T(8,128)} %bitcast.3, f32[2,64,2,8,512]{4,3,2,1,0:T(8,128)} %src_hbm.1), custom_call_target="tpu_custom_call" | custom-call | flops 20000000 | bytes 24000000 | tf_op jit(solution)/shard_map/slopes/pallas_call | solution.py:250
  10.6 6.8 %all-to-all-start = ((f32[8,24,8,128]{3,2,1,0:T(8,128)}), f32[8,24,8,128]{3,2,1,0:T(8,128)S(1)}, u32[]{:S(2)}, u32[]{:S(2)}) async-start(f32[8,24,8,128]{3,2,1,0:T(8,128)} %get-tuple-element.11), calls=%async_computation | async-start | bytes 1572864 | tf_op jit(solution)/shard_map/all_to_all | solution.py:603
  17.4 14.4 %particular.1 = (f32[2,64,5,8,128]{4,3,2,1,0:T(8,128)}, f32[2,64,8,128]{3,2,1,0:T(8,128)}) custom-call(s32[8]{0:T(128)} %slot_ref.5, f32[2,64,8,8,512]{4,3,2,1,0:T(8,128)} %bitcast.4, f32[2,64,5,8,128]{4,3,2,1,0:T(8,128)} %get-tuple-element.14.packed_hbm), custom_call_target="tpu_custom_call" | custom-call | flops 90000000 | bytes 24000000 | tf_op jit(solution)/shard_map/particular/pallas_call | solution.py:371
  31.8 0.0 all-to-all-done.all_hbm
  31.8 0.0 copy-start
  31.8 0.9 %copy-done = f32[8,24,8,128]{3,2,1,0:T(8,128)} copy-done((f32[8,24,8,128]{3,2,1,0:T(8,128)}, f32[8,24,8,128]{3,2,1,0:T(8,128)S(1)}, u32[]{:S(2)}) %copy-start) | copy-done | bytes 786456
  32.7 4.7 %pack.1 = f32[16,33,8,128]{3,2,1,0:T(8,128)} custom-call(s32[8]{0:T(128)} %slot_ref.5, f32[8,24,8,128]{3,2,1,0:T(8,128)} %copy-done, f32[24,5,8,128]{3,2,1,0:T(8,128)} %get-tuple-element.12.early_part, f32[24,8,128]{2,1,0:T(8,128)} %get-tuple-element.13.early_edge, f32[2,64,5,8,128]{4,3,2,1,0:T(8,128)} %get-tuple-element.15.part_hbm, ...), custom_call_target="tpu_custom_call" | custom-call | tf_op jit(solution)/shard_map/pack/pallas_call | solution.py:517
  37.4 35.8 %all_to_all.10 = f32[16,264,128]{2,1,0:T(8,128)} all-to-all(f32[16,264,128]{2,1,0:T(8,128)} %bitcast.6), channel_id=1, replica_groups=mesh['sub'=8,'ma'=16] {'ma'}, dimensions={0} | all-to-all | bytes 4325376 | tf_op jit(solution)/shard_map/all_to_all | solution.py:596
  73.2 3.5 %unpack.1 = f32[2,4,2,128,512]{4,3,2,1,0:T(8,128)} custom-call(f32[16,33,8,128]{3,2,1,0:T(8,128)} %bitcast.5), custom_call_target="tpu_custom_call" | custom-call | tf_op jit(solution)/shard_map/unpack/pallas_call | solution.py:579
Async XLA Ops:
  10.6 21.3 %all-to-all-start = ((f32[8,24,8,128]{3,2,1,0:T(8,128)}), f32[8,24,8,128]{3,2,1,0:T(8,128)S(1)}, u32[]{:S(2)}, u32[]{:S(2)}) async-start(f32[8,24,8,128]{3,2,1,0:T(8,128)} %get-tuple-element.11), calls=%async_computation | async-start | bytes 1572864 | tf_op jit(solution)/shard_map/all_to_all | solution.py:603
  31.8 0.9 %copy-start = (f32[8,24,8,128]{3,2,1,0:T(8,128)}, f32[8,24,8,128]{3,2,1,0:T(8,128)S(1)}, u32[]{:S(2)}) copy-start(f32[8,24,8,128]{3,2,1,0:T(8,128)S(1)} %all-to-all-done.all_hbm) | copy-start | bytes 2359300

commit v4 on v3

--- a/solution.py
+++ b/solution.py
@@ -86,6 +86,10 @@
 
 AHEAD = 8
 EARLY = 3
+PARTICULAR_MIB = 24
+PACK_MIB = 4
+UNPACK_MIB = 8
+KEPT = PACK + 1
 CHUNKS = FIELDS * BLOCKS
 
 
@@ -123,17 +127,14 @@
 
 
 def slope_kernel(
-    slot_ref, weight_ref, inv_hbm, src_hbm, packed_hbm, msg_hbm, part_hbm, edge_hbm,
-    inv_v, src_v, packed_v, e_v, msg_ref, part_v, edge_v, odd_v, inv_sem, src_sem, out_sem, msg_sem, early_sem
+    slot_ref, weight_ref, inv_hbm, src_hbm, packed_hbm, msg_hbm, part_hbm,
+    inv_v, src_v, packed_v, e_v, msg_ref, part_v, odd_v, inv_sem, src_sem, out_sem, msg_sem, early_sem
 ):
     copy = inverse_chunks(inv_hbm, inv_v, inv_sem)
     sources = [pltpu.make_async_copy(src_hbm.at[f], src_v.at[f], src_sem.at[f]) for f in range(FIELDS)]
     results = [pltpu.make_async_copy(packed_v.at[f], packed_hbm.at[f], out_sem.at[f]) for f in range(FIELDS)]
     rows = pl.ds(0, EARLY * PB)
-    early = [
-        pltpu.make_async_copy(part_v.at[0, rows], part_hbm, early_sem.at[0]),
-        pltpu.make_async_copy(edge_v.at[0, rows], edge_hbm, early_sem.at[1]),
-    ]
+    early = [pltpu.make_async_copy(part_v.at[0, rows], part_hbm, early_sem)]
     sources[0].start()
     start_all(copy, AHEAD)
     m = pair_wavenumber(slot_ref)
@@ -194,7 +195,7 @@
 
         def weigh_and_solve(block, carry):
             weigh(block, carry)
-            solve_block(f, inv_v, packed_v, block, small, odd_v, part_v, edge_v)
+            solve_block(f, inv_v, packed_v, block, small, odd_v, part_v)
             return carry
 
         if f == 0:
@@ -239,7 +240,22 @@
 SCALARS = pl.BlockSpec(memory_space=pltpu.SMEM)
 INVERSE_V = pltpu.VMEM((FIELDS, POINTS, POINTS // ROWS, ROWS, 512), F32)
 PACKED_V = pltpu.VMEM((FIELDS, POINTS, PACK, ROWS, LANES), F32)
-EDGE_V = pltpu.VMEM((FIELDS, POINTS, ROWS, LANES), F32)
+PART_V = pltpu.VMEM((FIELDS, POINTS, KEPT, ROWS, LANES), F32)
+SENT_V = pltpu.VMEM((GROUPS, SENT, ROWS, LANES), F32)
+IN_VMEM = pl.BlockSpec(memory_space=pltpu.VMEM)
+IN_HBM = pl.BlockSpec(memory_space=pltpu.HBM)
+
+
+def grant(mib):
+    return pltpu.CompilerParams(vmem_limit_bytes=mib * 2**20)
+
+
+def held(x):
+    return pltpu.with_memory_space_constraint(x, pltpu.VMEM)
+
+
+def far(x):
+    return pltpu.with_memory_space_constraint(x, pltpu.HBM)
 
 
 def dma(*shape):
@@ -250,12 +266,11 @@
     return pl.pallas_call(
         slope_kernel,
         in_specs=[SCALARS, SCALARS, ANY, ANY],
-        out_specs=[ANY] * 4,
+        out_specs=[ANY] * 3,
         out_shape=[
             jax.ShapeDtypeStruct((FIELDS, POINTS, PACK, ROWS, LANES), F32),
             jax.ShapeDtypeStruct((NSUB, FIELDS * MESSAGE, ROWS, LANES), F32),
-            jax.ShapeDtypeStruct((EARLY * PB, PACK, ROWS, LANES), F32),
-            jax.ShapeDtypeStruct((EARLY * PB, ROWS, LANES), F32),
+            jax.ShapeDtypeStruct((EARLY * PB, KEPT, ROWS, LANES), F32),
         ],
         scratch_shapes=[
             INVERSE_V,
@@ -263,14 +278,13 @@
             pltpu.VMEM((FIELDS, POINTS, PACK, ROWS, LANES), F32),
             pltpu.VMEM((2, POINTS // ROWS, 4, ROWS, LANES), F32),
             pltpu.VMEM((FIELDS * MESSAGE, ROWS, LANES), F32),
-            pltpu.VMEM((1, EARLY * PB, PACK, ROWS, LANES), F32),
-            pltpu.VMEM((1, EARLY * PB, ROWS, LANES), F32),
+            pltpu.VMEM((1, EARLY * PB, KEPT, ROWS, LANES), F32),
             pltpu.VMEM((3 * PB, ROWS, LANES), F32),
             dma(CHUNKS),
             dma(FIELDS),
             dma(FIELDS),
             dma(NSUB),
-            dma(2),
+            pltpu.SemaphoreType.DMA,
         ],
         cost_estimate=pl.CostEstimate(flops=20_000_000, bytes_accessed=24_000_000, transcendentals=0),
         name="slopes",
@@ -320,7 +334,7 @@
     return [[odd_v[3 * p], even[2 * p], odd_v[3 * p + 1], odd_v[3 * p + 2], even[2 * p + 1]] for p in range(PB)]
 
 
-def solve_block(f, inv_v, packed_v, block, small, odd_v, part_v, edge_v):
+def solve_block(f, inv_v, packed_v, block, small, odd_v, part_v):
     x = block_sums(f, inv_v, packed_v, block, small, odd_v)
     for p in range(PB):
         at = block * PB + p
@@ -328,27 +342,20 @@
             part_v[f, at, v] = x[p][v]
         for b in range(4):
             lanes = slice(b * LANES, (b + 1) * LANES)
-            edge_v[f, at, 2 * b:2 * b + 1, :] = inv_v[f, at, 0, 0:1, lanes]
-            edge_v[f, at, 2 * b + 1:2 * b + 2, :] = inv_v[f, at, POINTS // ROWS - 1, ROWS - 1:ROWS, lanes]
+            part_v[f, at, PACK, 2 * b:2 * b + 1, :] = inv_v[f, at, 0, 0:1, lanes]
+            part_v[f, at, PACK, 2 * b + 1:2 * b + 2, :] = inv_v[f, at, POINTS // ROWS - 1, ROWS - 1:ROWS, lanes]
 
 
 def particular_kernel(
-    slot_ref, inv_hbm, packed_hbm, part_hbm, edge_hbm, inv_v, packed_v, part_v, edge_v, odd_v, inv_sem, src_sem, part_sem, edge_sem
+    slot_ref, inv_hbm, packed_hbm, early_hbm, part_v, inv_v, packed_v, odd_v, inv_sem, src_sem, early_sem
 ):
     copy = inverse_chunks(inv_hbm, inv_v, inv_sem)
     sources = [pltpu.make_async_copy(packed_hbm.at[f], packed_v.at[f], src_sem.at[f]) for f in range(FIELDS)]
+    early = pltpu.make_async_copy(early_hbm, part_v.at[0, pl.ds(0, EARLY * PB)], early_sem)
     sources[0].start()
     start_all(copy, AHEAD, EARLY)
+    early.start()
     small = pair_wavenumber(slot_ref) < LANES
-
-    def part_copy(i):
-        f, rows = i // BLOCKS, pl.ds(lax.rem(i, BLOCKS) * PB, PB)
-        return pltpu.make_async_copy(part_v.at[f, rows], part_hbm.at[f, rows], part_sem.at[i])
-
-    edges = []
-    for f in range(FIELDS):
-        late = pl.ds(EARLY * PB if f == 0 else 0, POINTS - (EARLY * PB if f == 0 else 0))
-        edges.append(pltpu.make_async_copy(edge_v.at[f, late], edge_hbm.at[f, late], edge_sem.at[f]))
     for f in range(FIELDS):
         sources[f].wait()
         if f + 1 < FIELDS:
@@ -356,40 +363,31 @@
 
         def step(block, carry):
             next_chunk(copy, f * BLOCKS + block)
-            solve_block(f, inv_v, packed_v, block, small, odd_v, part_v, edge_v)
-            part_copy(f * BLOCKS + block).start()
+            solve_block(f, inv_v, packed_v, block, small, odd_v, part_v)
             return carry
 
         lax.fori_loop(EARLY if f == 0 else 0, BLOCKS, step, 0)
-        edges[f].start()
-    wait_all(part_copy, CHUNKS, EARLY)
-    for edge in edges:
-        edge.wait()
-
-
-def particular(slot, inverse, packed):
+    early.wait()
+
+
+def particular(slot, inverse, packed, early):
     return pl.pallas_call(
         particular_kernel,
-        in_specs=[SCALARS, ANY, ANY],
-        out_specs=[ANY, ANY],
-        out_shape=[
-            jax.ShapeDtypeStruct((FIELDS, POINTS, PACK, ROWS, LANES), F32),
-            jax.ShapeDtypeStruct((FIELDS, POINTS, ROWS, LANES), F32),
-        ],
+        in_specs=[SCALARS] + [IN_HBM] * 3,
+        out_specs=IN_VMEM,
+        out_shape=PART_V,
         scratch_shapes=[
             INVERSE_V,
             PACKED_V,
-            PACKED_V,
-            EDGE_V,
             pltpu.VMEM((3 * PB, ROWS, LANES), F32),
             dma(CHUNKS),
             dma(FIELDS),
-            dma(CHUNKS),
-            dma(FIELDS),
+            pltpu.SemaphoreType.DMA,
         ],
+        compiler_params=grant(PARTICULAR_MIB),
         cost_estimate=pl.CostEstimate(flops=90_000_000, bytes_accessed=24_000_000, transcendentals=0),
         name="particular",
-    )(slot, inverse, packed)
+    )(slot, far(inverse), far(packed), far(early))
 
 
 def solve_interface(f, all_v, u_v, small):
@@ -434,56 +432,16 @@
 PER = PB // NEAR
 
 
-def pack_kernel(
-    slot_ref, all_hbm, early_part, early_edge, part_hbm, edge_hbm, out_hbm,
-    all_v, u_v, part_v, edge_v, out_v, all_sem, part_sem, edge_sem, early_sem, out_sem
-):
-    messages = pltpu.make_async_copy(all_hbm, all_v, all_sem)
-    messages.start()
-    rows = pl.ds(0, EARLY * PB)
-    late = pl.ds(EARLY * PB, POINTS - EARLY * PB)
-    edges = [
-        pltpu.make_async_copy(early_edge, edge_v.at[0, rows], edge_sem.at[0]),
-        pltpu.make_async_copy(edge_hbm.at[0, late], edge_v.at[0, late], edge_sem.at[1]),
-        pltpu.make_async_copy(edge_hbm.at[1], edge_v.at[1], edge_sem.at[2]),
-    ]
-    for edge in edges:
-        edge.start()
-
-    def first_copy(i):
-        rows = pl.ds(i * PB, PB)
-        return pltpu.make_async_copy(early_part.at[rows], part_v.at[0, rows], early_sem.at[i])
-
-    def late_copy(i):
-        rows = pl.ds(i * PB, PB)
-        return pltpu.make_async_copy(part_hbm.at[0, rows], part_v.at[0, rows], early_sem.at[i])
-
-    def part_copy(i):
-        rows = pl.ds(i * PB, PB)
-        return pltpu.make_async_copy(part_hbm.at[1, rows], part_v.at[1, rows], part_sem.at[i])
-
-    start_all(first_copy, EARLY)
-    start_all(part_copy, EARLY)
-    start_all(late_copy, BLOCKS - EARLY, EARLY)
-    start_all(part_copy, BLOCKS - EARLY, EARLY)
+def pack_kernel(slot_ref, all_v, part_v, out_v, u_v):
     m = pair_wavenumber(slot_ref)
     lane = lane_iota()
     even = row_iota() % 2 == 0
     small = m < LANES
-    messages.wait()
     for f in range(FIELDS):
         solve_interface(f, all_v, u_v, small)
-    for edge in edges:
-        edge.wait()
     sub = lax.axis_index("sub")
 
-    def out_copy(i):
-        rows = pl.ds(i * PER, PER)
-        return pltpu.make_async_copy(out_v.at[rows], out_hbm.at[rows], out_sem.at[i])
-
     def step(block, carry):
-        late_copy(block).wait()
-        part_copy(block).wait()
         for d in range(PER):
             dest = block * PER + d
             extra = jnp.where(lane == FIELDS * NEAR, m.astype(F32), 0.0)
@@ -492,8 +450,8 @@
                 u_top = [u_v[sub + 1, f, v] for v in range(PACK)]
                 for k in range(NEAR):
                     p = block * PB + d * NEAR + k
-                    low = [edge_v[f, p, pl.ds(2 * b, ROWS, stride=0), :] for b in range(4)]
-                    top = [edge_v[f, p, pl.ds(2 * b + 1, ROWS, stride=0), :] for b in range(4)]
+                    low = [part_v[f, p, PACK, pl.ds(2 * b, ROWS, stride=0), :] for b in range(4)]
+                    top = [part_v[f, p, PACK, pl.ds(2 * b + 1, ROWS, stride=0), :] for b in range(4)]
                     low = [low[1], low[2], low[3], low[3], jnp.where(small, low[0], low[2])]
                     top = [top[1], top[2], top[3], top[3], jnp.where(small, top[0], top[2])]
                     x = [part_v[f, p, v] + u_low[v] * low[v] + u_top[v] * top[v] for v in range(PACK)]
@@ -503,57 +461,36 @@
                         out_v[dest, at * 4 + b] = s[b]
                     extra = jnp.where(lane == at, spare, extra)
             out_v[dest, SENT - 1] = extra
-        out_copy(block).start()
         return carry
 
     lax.fori_loop(0, BLOCKS, step, 0)
-    wait_all(out_copy, BLOCKS)
-
-
-SENT_V = pltpu.VMEM((GROUPS, SENT, ROWS, LANES), F32)
-
-
-def pack(slot, messages, early_part, early_edge, part, edges):
+
+
+def pack(slot, messages, part):
     return pl.pallas_call(
         pack_kernel,
-        in_specs=[SCALARS] + [ANY] * 5,
-        out_specs=ANY,
-        out_shape=jax.ShapeDtypeStruct((GROUPS, SENT, ROWS, LANES), F32),
-        scratch_shapes=[
-            pltpu.VMEM((NSUB, FIELDS * MESSAGE, ROWS, LANES), F32),
-            pltpu.VMEM((NSUB + 1, FIELDS, PACK, ROWS, LANES), F32),
-            PACKED_V,
-            EDGE_V,
-            SENT_V,
-            pltpu.SemaphoreType.DMA,
-            dma(BLOCKS),
-            dma(3),
-            dma(BLOCKS),
-            dma(BLOCKS),
-        ],
+        in_specs=[SCALARS] + [IN_VMEM] * 2,
+        out_specs=IN_VMEM,
+        out_shape=SENT_V,
+        scratch_shapes=[pltpu.VMEM((NSUB + 1, FIELDS, PACK, ROWS, LANES), F32)],
+        compiler_params=grant(PACK_MIB),
         name="pack",
-    )(slot, messages, early_part, early_edge, part, edges)
+    )(slot, held(messages), held(part))
 
 
 STEPS = 8
 FROM = GROUPS // STEPS
 
 
-def unpack_kernel(in_hbm, out_hbm, in_v, out_v, in_sem, out_sem):
-    def in_copy(i):
-        rows = pl.ds(i * FROM, FROM)
-        return pltpu.make_async_copy(in_hbm.at[rows], in_v.at[rows], in_sem.at[i])
-
+def unpack_kernel(in_v, out_hbm, out_v, out_sem):
     def out_copy(i):
         rows = pl.ds(pl.multiple_of(i * FROM * ROWS, ROWS), FROM * ROWS)
         return pltpu.make_async_copy(out_v.at[:, :, :, rows, :], out_hbm.at[:, :, :, rows, :], out_sem.at[i])
 
-    start_all(in_copy, STEPS)
     lane = lane_iota()
     even = row_iota() % 2 == 0
 
     def step(i, carry):
-        in_copy(i).wait()
         for d in range(FROM):
             g = i * FROM + d
             extras = in_v[g, SENT - 1]
@@ -578,17 +515,13 @@
 def unpack(received):
     return pl.pallas_call(
         unpack_kernel,
-        in_specs=[ANY],
+        in_specs=[IN_VMEM],
         out_specs=ANY,
         out_shape=jax.ShapeDtypeStruct((FIELDS, NEAR, 2, GROUPS * ROWS, 512), F32),
-        scratch_shapes=[
-            SENT_V,
-            pltpu.VMEM((FIELDS, NEAR, 2, GROUPS * ROWS, 512), F32),
-            dma(STEPS),
-            dma(STEPS),
-        ],
+        scratch_shapes=[pltpu.VMEM((FIELDS, NEAR, 2, GROUPS * ROWS, 512), F32), dma(STEPS)],
+        compiler_params=grant(UNPACK_MIB),
         name="unpack",
-    )(received)
+    )(held(received))
 
 
 def over_ma(sent):
@@ -599,10 +532,10 @@
 
 def body(forcing, slot_wavenumber, inverse, edge_weights):
     inverse = inverse.reshape(FIELDS, POINTS, POINTS // ROWS, ROWS, 512)
-    packed, messages, early_part, early_edge = slopes(slot_wavenumber, edge_weights, inverse, forcing)
+    packed, messages, early = slopes(slot_wavenumber, edge_weights, inverse, forcing)
     messages = lax.all_to_all(messages, "sub", split_axis=0, concat_axis=0, tiled=True)
-    part, edges = particular(slot_wavenumber, inverse, packed)
-    sent = pack(slot_wavenumber, messages, early_part, early_edge, part, edges)
+    part = particular(slot_wavenumber, inverse, packed, early)
+    sent = pack(slot_wavenumber, messages, part)
     return unpack(over_ma(sent))
 
 

time: 77 us -> 71.9 us (0.934)
  Pallas kernels: 33.2 us -> 29.3 us
  local copies, waits for them, and re-layouts: 0.88 us -> 0.01 us
    pallas_call x3, Pallas kernels: 22.7 us -> 18.6 us  [the longest x1 13.3 us: particular(): pl.pallas_call(particular_kernel, in_specs=[SCALARS] + [IN_HBM] * 3, out_...]
    unnamed x2, local copies, waits for them, and re-layouts: 0.88 us -> 0.01 us
where the time goes in v4:
time: 71.9 us; the launch traced here: 71.7 us
  blocking collectives  35.5 us (49%)
  Pallas kernels  29.3 us (41%)
  starting transfers between devices  6.81 us (9%)
    all_to_all x1, blocking collectives, over_ma(): lax.all_to_all(flat, 'ma', split_axis=0, concat_axis=0, tiled=True)  35.5 us
    pallas_call x1, Pallas kernels, particular(): pl.pallas_call(particular_kernel, in_specs=[SCALARS] + [IN_HBM] * 3, out_...  13.3 us
    pallas_call x1, Pallas kernels, slopes(): pl.pallas_call(slope_kernel, in_specs=[SCALARS, SCALARS, ANY, ANY], out_s...  10.7 us
    all_to_all x1, starting transfers between devices, body(): lax.all_to_all(messages, 'sub', split_axis=0, concat_axis=0, tiled=True)  6.81 us
    pallas_call x1, Pallas kernels, pack(): pl.pallas_call(pack_kernel, in_specs=[SCALARS] + [IN_VMEM] * 2, out_specs...  2.86 us
    pallas_call x1, Pallas kernels, unpack(): pl.pallas_call(unpack_kernel, in_specs=[IN_VMEM], out_specs=ANY, out_shap...  2.5 us
  transfers between devices with their start and end apart: 1, of which 0 were waited for; matrix products, arithmetic and copies ran while one was open for 0% of the time, Pallas kernels for 19%

profile of v4, /device:TPU:1, one launch (start us, length us, event | category | flops | bytes accessed | tf_op | source)
XLA Modules:
  0.0 71.7 jit_solution(3202267072528356373)
XLA Ops:
  0.0 0.0 copy-start
  0.0 10.7 %slopes.1 = (f32[2,64,5,8,128]{4,3,2,1,0:T(8,128)}, f32[8,24,8,128]{3,2,1,0:T(8,128)}, f32[24,6,8,128]{3,2,1,0:T(8,128)}) custom-call(s32[8]{0:T(128)} %slot_ref.5, f32[1,2,64]{2,1,0:T(2,128)} %weight_ref.1, f32[2,64,8,8,512]{4,3,2,1,0:T(8,128)} %bitcast.5, f32[2,64,2,8,512]{4,3,2,1,0:T(8,128)} %src_hbm.1), custom_call_target="tpu_custom_call" | custom-call | flops 20000000 | bytes 24000000 | tf_op jit(solution)/shard_map/slopes/pallas_call | solution.py:266
  10.7 6.8 %all-to-all-start = ((f32[8,24,8,128]{3,2,1,0:T(8,128)}), f32[8,24,8,128]{3,2,1,0:T(8,128)}, u32[]{:S(2)}, u32[]{:S(2)}) async-start(f32[8,24,8,128]{3,2,1,0:T(8,128)} %get-tuple-element.8), calls=%async_computation | async-start | bytes 1572864 | tf_op jit(solution)/shard_map/all_to_all | solution.py:536
  17.5 0.0 copy-done
  17.5 13.3 %particular.1.part_v = f32[2,64,6,8,128]{4,3,2,1,0:T(8,128)S(1)} custom-call(s32[8]{0:T(128)S(1)} %copy-done, f32[2,64,8,8,512]{4,3,2,1,0:T(8,128)} %bitcast.6, f32[2,64,5,8,128]{4,3,2,1,0:T(8,128)} %get-tuple-element.9.packed_hbm, f32[24,6,8,128]{3,2,1,0:T(8,128)} %get-tuple-element.10.early_hbm), custom_call_target="tpu_custom_call" | custom-call | flops 90000000 | bytes 24000000 | tf_op jit(solution)/shard_map/particular/pallas_call | solution.py:374
  30.8 0.0 all-to-all-done.all_v
  30.8 2.9 %pack.1 = f32[16,33,8,128]{3,2,1,0:T(8,128)S(1)} custom-call(s32[8]{0:T(128)S(1)} %copy-done, f32[8,24,8,128]{3,2,1,0:T(8,128)} %all-to-all-done.all_v, f32[2,64,6,8,128]{4,3,2,1,0:T(8,128)S(1)} %particular.1.part_v), custom_call_target="tpu_custom_call" | custom-call | tf_op jit(solution)/shard_map/pack/pallas_call | solution.py:470
  33.7 35.5 %all_to_all.10 = f32[16,264,128]{2,1,0:T(8,128)S(1)} all-to-all(f32[16,264,128]{2,1,0:T(8,128)S(1)} %bitcast.3), channel_id=1, replica_groups=mesh['sub'=8,'ma'=16] {'ma'}, dimensions={0} | all-to-all | bytes 4325376 | tf_op jit(solution)/shard_map/all_to_all | solution.py:529
  69.2 2.5 %unpack.1 = f32[2,4,2,128,512]{4,3,2,1,0:T(8,128)} custom-call(f32[16,33,8,128]{3,2,1,0:T(8,128)S(1)} %bitcast.4), custom_call_target="tpu_custom_call" | custom-call | tf_op jit(solution)/shard_map/unpack/pallas_call | solution.py:516
Async XLA Ops:
  0.0 17.5 %copy-start = (s32[8]{0:T(128)S(1)}, s32[8]{0:T(128)}, u32[]{:S(2)}) copy-start(s32[8]{0:T(128)} %slot_ref.5) | copy-start | bytes 100
  10.7 20.1 %all-to-all-start = ((f32[8,24,8,128]{3,2,1,0:T(8,128)}), f32[8,24,8,128]{3,2,1,0:T(8,128)}, u32[]{:S(2)}, u32[]{:S(2)}) async-start(f32[8,24,8,128]{3,2,1,0:T(8,128)} %get-tuple-element.8), calls=%async_computation | async-start | bytes 1572864 | tf_op jit(solution)/shard_map/all_to_all | solution.py:536
